TPU v7x, 32 devices: a whole 2x2x4 slice. The times are simulated.
32 devices in a mesh: dp: 4 (over x, core), expert: 8 (over z, y).
Axes of the slice: x: 2, y: 2, z: 4, core: 2. Of those that a mesh axis runs over, the one named last changes fastest.
Arguments:
- tokens: bfloat16 [4096, 2560], P(('dp', 'expert')), parts along dimension 0, may hold values from -6 to 6
- expert_ids: int32 [4096, 2], P(('dp', 'expert')), parts along dimension 0, may hold values from 0 to 15, all different within a row; in each aligned block of 128 rows (0 to 127, 128 to 255, ...) at most 20 rows name the same one
- gate_weights: float32 [4096, 2], P(('dp', 'expert')), parts along dimension 0, may hold values from 0.1 to 1
- w_gate: bfloat16 [2560, 12288], P(None, 'expert'), may hold values from -0.125 to 0.125
- w_up: bfloat16 [2560, 12288], P(None, 'expert'), may hold values from -0.125 to 0.125
- w_down: bfloat16 [12288, 2560], P('expert'), may hold values from -0.21875 to 0.21875
Outputs:
- moe_out: bfloat16 [4096, 2560], P(('dp', 'expert')), parts along dimension 0
There are 4 independent parts, one for each index of `dp`. A program takes and returns all parts, laid end to end along the dimension named above; an argument that names none is the same for every part. Nothing has to cross between parts.
Inputs may be any that keep to these rules, and one draw needn't show every extreme that they name: `expert_ids`: each row names 2 different experts; in each aligned block of 128 rows (the rows of one device) no expert is named by more than 20 rows, a bound that some block reaches.
All inputs are finite; a program needn't handle non-finite values.
Results may differ from a plain program's by a relative error of at most 0.01.
Values may be sent and summed in bfloat16 or wider, within the bound.
No kernel may reach another device: no remote copies, remote signals or barrier semaphores. Data moves between devices by JAX's collectives and lax.ppermute only.
A program may use at most 64 MiB of HBM per device.

v0:
```python
import jax
import jax.numpy as jnp
from jax import lax
from jax.sharding import PartitionSpec as P

EXPERTS = 16
CAP = 20


def partner(value, axis, stride):
    return lax.ppermute(value, axis, [(i, i ^ 1 << stride) for i in range(lax.axis_size(axis))])


def expert_part(block_rows, gate_cols, up_cols, down_rows):
    gate_act = jnp.dot(block_rows, gate_cols, preferred_element_type=jnp.float32)
    up_act = jnp.dot(block_rows, up_cols, preferred_element_type=jnp.float32)
    hidden = (jax.nn.silu(gate_act) * up_act).astype(jnp.bfloat16)
    return jnp.dot(hidden, down_rows, preferred_element_type=jnp.float32).astype(jnp.bfloat16)


def local_experts(arrived, members, local_count, w_gate, w_up, w_down):
    model_width = arrived.shape[1]
    width_each = w_gate.shape[1] // local_count
    per_expert = arrived.shape[0] // (members * local_count)
    grouped = arrived.reshape(members, local_count, per_expert, model_width)
    pieces = []
    for member in range(local_count):
        lower_col = member * width_each
        rows_now = grouped[:, member].reshape(-1, model_width)
        computed = expert_part(
            rows_now,
            w_gate[:, lower_col : lower_col + width_each],
            w_up[:, lower_col : lower_col + width_each],
            w_down[lower_col : lower_col + width_each],
        )
        pieces.append(computed.reshape(members, 1, per_expert, model_width))
    return jnp.concatenate(pieces, axis=1).reshape(-1, model_width)


def per_device(tokens, expert_ids, gate_weights, w_gate, w_up, w_down):
    members = lax.axis_size("expert")
    tok_rows, model_width = tokens.shape
    pick_count = expert_ids.shape[1]
    local_count = max(1, EXPERTS // members)
    halves = members * local_count // EXPERTS
    flat_ids = expert_ids.reshape(-1)
    pick_total = flat_ids.shape[0]
    one_hot = (flat_ids[:, None] == jnp.arange(EXPERTS, dtype=jnp.int32)[None, :]).astype(
        jnp.float32
    )
    pick_iota = jnp.arange(pick_total, dtype=jnp.int32)
    lower_tri = (pick_iota[:, None] > pick_iota[None, :]).astype(jnp.float32)
    earlier = jnp.dot(
        lower_tri, one_hot, precision=lax.Precision.HIGHEST, preferred_element_type=jnp.float32
    )
    slot_index = jnp.sum(earlier * one_hot, axis=1).astype(jnp.int32)
    position = flat_ids * CAP + slot_index
    token_of = pick_iota // pick_count
    slot_iota = jnp.arange(EXPERTS * CAP, dtype=jnp.int32)
    pick_slot = (slot_iota[:, None] == position[None, :]).astype(jnp.bfloat16)
    pick_token = (token_of[:, None] == jnp.arange(tok_rows, dtype=jnp.int32)[None, :]).astype(
        jnp.bfloat16
    )
    chooser = jnp.dot(pick_slot, pick_token, preferred_element_type=jnp.float32).astype(
        jnp.bfloat16
    )
    slot_rows = jnp.dot(chooser, tokens, preferred_element_type=jnp.float32).astype(jnp.bfloat16)
    arrived = lax.all_to_all(slot_rows, "expert", split_axis=0, concat_axis=0, tiled=True)
    if halves == 1:
        expert_out = local_experts(arrived, members, local_count, w_gate, w_up, w_down)
    else:
        partner_rows = partner(arrived, "expert", 0)
        own_count = arrived.shape[0]
        computed = expert_part(
            jnp.concatenate([arrived, partner_rows], axis=0), w_gate, w_up, w_down
        )
        returned = partner(computed[own_count:], "expert", 0)
        expert_out = (
            computed[:own_count].astype(jnp.float32) + returned.astype(jnp.float32)
        ).astype(jnp.bfloat16)
    returned_rows = lax.all_to_all(expert_out, "expert", split_axis=0, concat_axis=0, tiled=True)
    weighted_picks = pick_token.astype(jnp.float32).T * gate_weights.reshape(-1)[None, :]
    mixer = jnp.dot(
        weighted_picks,
        pick_slot.astype(jnp.float32).T,
        precision=lax.Precision.HIGHEST,
        preferred_element_type=jnp.float32,
    )
    mixed = jnp.dot(
        mixer,
        returned_rows.astype(jnp.float32),
        precision=lax.Precision.HIGHEST,
        preferred_element_type=jnp.float32,
    )
    return mixed.astype(jnp.bfloat16)


def solution(mesh):
    in_specs = (
        P(("dp", "expert"), None),
        P(("dp", "expert"), None),
        P(("dp", "expert"), None),
        P(None, "expert"),
        P(None, "expert"),
        P("expert", None),
    )
    out_specs = P(("dp", "expert"), None)
    return jax.shard_map(
        per_device, mesh=mesh, in_specs=in_specs, out_specs=out_specs, check_vma=False
    )
```

profile of v0, /device:TPU:0, one launch (start us, length us, event | category | flops | bytes accessed | tf_op | source)
XLA Modules:
  0.0 115.1 jit_solution(7890752536810641314)
XLA Ops:
  0.0 0.0 copy-start
  0.0 0.9 copy.21
  0.9 0.1 reshape.43
  1.0 0.2 fusion.30
  1.2 0.0 copy-done
  1.2 0.9 convolution_convert_fusion
  2.1 46.1 %all_to_all.21 = bf16[8,40,2560]{2,1,0:T(8,128)(2,1)S(1)} all-to-all(bf16[8,40,2560]{2,1,0:T(8,128)(2,1)S(1)} %bitcast.18), channel_id=1, replica_groups=mesh['dp'=4,'expert'=8] {'expert'}, dimensions={0} | all-to-all | bytes 3276800 | tf_op jit(solution)/shard_map/all_to_all | solution.py:68
  48.2 0.5 copy.22
  48.7 0.1 fusion.62
  48.8 0.2 copy.23
  49.1 0.2 reshape_squeeze.6
  49.2 3.7 %fusion.10 = f32[160,768]{1,0:T(8,128)} fusion(bf16[160,2560]{1,0:T(8,128)(2,1)S(1)} %reshape_squeeze.6, bf16[2560,1536]{1,0:T(8,128)(2,1)} %param.9), kind=kOutput, calls=%fused_computation.11 | convolution fusion | flops 629145600 | bytes 5242880 | tf_op jit(solution)/shard_map/dot_general | solution.py:15
  52.9 5.4 %fusion.12 = bf16[160,2560]{1,0:T(8,128)(2,1)S(1)} fusion(bf16[1536,2560]{1,0:T(8,128)(2,1)} %param.11, bf16[160,2560]{1,0:T(8,128)(2,1)S(1)} %reshape_squeeze.6, bf16[2560,1536]{1,0:T(8,128)(2,1)} %param.10, f32[160,768]{1,0:T(8,128)} %fusion.10), kind=kOutput, calls=%fused_computation.13 | convolution fusion | flops 1259438080 | bytes 9994240 | tf_op jit(solution)/shard_map/dot_general | solution.py:18
  58.3 0.2 reshape.45
  58.5 0.2 copy.24
  58.8 0.2 reshape_squeeze.7
  58.9 2.9 %fusion.4 = f32[160,768]{1,0:T(8,128)S(1)} fusion(bf16[160,2560]{1,0:T(8,128)(2,1)S(1)} %reshape_squeeze.7, bf16[2560,1536]{1,0:T(8,128)(2,1)} %param.9), kind=kOutput, calls=%fused_computation.5 | convolution fusion | flops 629145600 | bytes 5242880 | tf_op jit(solution)/shard_map/dot_general | solution.py:15
  61.9 6.2 %fusion.15 = bf16[160,2560]{1,0:T(8,128)(2,1)} fusion(bf16[1536,2560]{1,0:T(8,128)(2,1)} %param.11, bf16[160,2560]{1,0:T(8,128)(2,1)S(1)} %reshape_squeeze.7, bf16[2560,1536]{1,0:T(8,128)(2,1)} %param.10, f32[160,768]{1,0:T(8,128)S(1)} %fusion.4), kind=kOutput, calls=%fused_computation.14 | convolution fusion | flops 1259438080 | bytes 9994240 | tf_op jit(solution)/shard_map/dot_general | solution.py:18
  68.0 1.3 %reshape.46 = bf16[8,1,20,2560]{3,2,0,1:T(8,128)(2,1)S(1)} reshape(bf16[160,2560]{1,0:T(8,128)(2,1)} %fusion.15) | data formatting | bytes 1638400 | tf_op jit(solution)/shard_map/reshape | solution.py:36
  69.3 0.2 pad_maximum_fusion
  69.6 0.5 copy.25
  70.0 0.0 copy-start.1
  70.1 1.6 %copy.26 = bf16[8,40,2560]{2,1,0:T(8,128)(2,1)} copy(bf16[8,40,2560]{2,0,1:T(8,128)(2,1)S(1)} %bitcast.15) | data formatting | bytes 3276800 | tf_op jit(solution)/shard_map/all_to_all | solution.py:81
  71.7 3.6 %all-to-all-start.1 = ((bf16[8,40,2560]{2,1,0:T(8,128)(2,1)}), bf16[8,40,2560]{2,1,0:T(8,128)(2,1)S(1)}, u32[]{:S(2)}, u32[]{:S(2)}) async-start(bf16[8,40,2560]{2,1,0:T(8,128)(2,1)} %copy.26), calls=%async_computation.1 | async-start | bytes 3276800 | tf_op jit(solution)/shard_map/all_to_all | solution.py:81
  75.3 0.0 copy-done.1
  75.3 0.1 copy.20
  75.4 0.1 mul.36
  75.6 0.3 fusion.45
  75.9 37.1 %all-to-all-done.1 = bf16[8,40,2560]{2,1,0:T(8,128)(2,1)S(1)} async-done(((bf16[8,40,2560]{2,1,0:T(8,128)(2,1)}), bf16[8,40,2560]{2,1,0:T(8,128)(2,1)S(1)}, u32[]{:S(2)}, u32[]{:S(2)}) %all-to-all-start.1) | async-done | bytes 1638432 | tf_op jit(solution)/shard_map/all_to_all | solution.py:81
  113.0 2.1 %convolution_convert_fusion.1 = bf16[128,2560]{1,0:T(8,128)(2,1)} fusion(f32[128,320]{0,1:T(8,128)S(1)} %fusion.45, bf16[320,2560]{1,0:T(8,128)(2,1)S(1)} %bitcast.16), kind=kOutput, calls=%fused_computation.15 | convolution fusion | flops 1258618880 | bytes 2457600 | tf_op jit(solution)/shard_map/dot_general | solution.py:89
  (1 shorter events, 0.0 us)
Async XLA Ops:
  0.0 1.2 %copy-start = (bf16[128,2560]{1,0:T(8,128)(2,1)S(1)}, bf16[128,2560]{1,0:T(8,128)(2,1)}, u32[]{:S(2)}) copy-start(bf16[128,2560]{1,0:T(8,128)(2,1)} %param.6) | copy-start | bytes 1966084
  70.0 5.3 %copy-start.1 = (f32[128,2]{0,1:T(2,128)S(1)}, f32[128,2]{0,1:T(2,128)}, u32[]{:S(2)}) copy-start(f32[128,2]{0,1:T(2,128)} %param.8) | copy-start | bytes 3076
  71.7 41.3 %all-to-all-start.1 = ((bf16[8,40,2560]{2,1,0:T(8,128)(2,1)}), bf16[8,40,2560]{2,1,0:T(8,128)(2,1)S(1)}, u32[]{:S(2)}, u32[]{:S(2)}) async-start(bf16[8,40,2560]{2,1,0:T(8,128)(2,1)} %copy.26), calls=%async_computation.1 | async-start | bytes 3276800 | tf_op jit(solution)/shard_map/all_to_all | solution.py:81
where the time goes:
time: 115 us
  blocking collectives  46.1 us (40%)
  waiting for transfers between devices  37.1 us (32%)
  matrix products  21.7 us (19%)
  local copies, waits for them, and re-layouts  6.25 us (5%)
  starting transfers between devices  3.58 us (3%)
    all_to_all x1, blocking collectives, per_device(): lax.all_to_all(slot_rows, 'expert', split_axis=0, concat_axis=0, tiled=True)  46.1 us
    all_to_all x1, waiting for transfers between devices, per_device(): lax.all_to_all(expert_out, 'expert', split_axis=0, concat_axis=0, tiled=T...  37.1 us
    dot_general x2, matrix products, expert_part(): jnp.dot(hidden, down_rows, preferred_element_type=jnp.float32)  11.6 us
    dot_general x2, matrix products, expert_part(): jnp.dot(block_rows, gate_cols, preferred_element_type=jnp.float32)  6.62 us
    all_to_all x1, starting transfers between devices, per_device(): lax.all_to_all(expert_out, 'expert', split_axis=0, concat_axis=0, tiled=T...  3.58 us
  transfers between devices with their start and end apart: 1, of which 1 were waited for; matrix products, arithmetic and copies ran while one was open for 0% of the time, Pallas kernels for 0%

commit v1 on v0

v1 whole, which is shorter than its diff:
```python
import functools

import jax
import jax.numpy as jnp
from jax import lax
from jax.experimental import pallas as pl
from jax.experimental.pallas import tpu as pltpu
from jax.sharding import PartitionSpec as P


EXPERTS = 16
CAP = 20


VMEM = pltpu.VMEM


def partner(value, axis, stride):
    return lax.ppermute(value, axis, [(i, i ^ 1 << stride) for i in range(lax.axis_size(axis))])


def expert_part(block_rows, gate_cols, up_cols, down_rows):
    gate_act = jnp.dot(block_rows, gate_cols, preferred_element_type=jnp.float32)
    up_act = jnp.dot(block_rows, up_cols, preferred_element_type=jnp.float32)
    hidden = (jax.nn.silu(gate_act) * up_act).astype(jnp.bfloat16)
    return jnp.dot(hidden, down_rows, preferred_element_type=jnp.float32).astype(jnp.bfloat16)


def split_experts(tokens, expert_ids, gate_weights, w_gate, w_up, w_down):
    tok_rows = tokens.shape[0]
    pick_count = expert_ids.shape[1]
    flat_ids = expert_ids.reshape(-1)
    pick_total = flat_ids.shape[0]
    one_hot = (flat_ids[:, None] == jnp.arange(EXPERTS, dtype=jnp.int32)[None, :]).astype(
        jnp.float32
    )
    pick_iota = jnp.arange(pick_total, dtype=jnp.int32)
    lower_tri = (pick_iota[:, None] > pick_iota[None, :]).astype(jnp.float32)
    earlier = jnp.dot(
        lower_tri, one_hot, precision=lax.Precision.HIGHEST, preferred_element_type=jnp.float32
    )
    slot_index = jnp.sum(earlier * one_hot, axis=1).astype(jnp.int32)
    position = flat_ids * CAP + slot_index
    token_of = pick_iota // pick_count
    slot_iota = jnp.arange(EXPERTS * CAP, dtype=jnp.int32)
    pick_slot = (slot_iota[:, None] == position[None, :]).astype(jnp.bfloat16)
    pick_token = (token_of[:, None] == jnp.arange(tok_rows, dtype=jnp.int32)[None, :]).astype(
        jnp.bfloat16
    )
    chooser = jnp.dot(pick_slot, pick_token, preferred_element_type=jnp.float32).astype(
        jnp.bfloat16
    )
    slot_rows = jnp.dot(chooser, tokens, preferred_element_type=jnp.float32).astype(jnp.bfloat16)
    arrived = lax.all_to_all(slot_rows, "expert", split_axis=0, concat_axis=0, tiled=True)
    partner_rows = partner(arrived, "expert", 0)
    own_count = arrived.shape[0]
    computed = expert_part(jnp.concatenate([arrived, partner_rows], axis=0), w_gate, w_up, w_down)
    returned = partner(computed[own_count:], "expert", 0)
    expert_out = (
        computed[:own_count].astype(jnp.float32) + returned.astype(jnp.float32)
    ).astype(jnp.bfloat16)
    returned_rows = lax.all_to_all(expert_out, "expert", split_axis=0, concat_axis=0, tiled=True)
    weighted_picks = pick_token.astype(jnp.float32).T * gate_weights.reshape(-1)[None, :]
    mixer = jnp.dot(
        weighted_picks,
        pick_slot.astype(jnp.float32).T,
        precision=lax.Precision.HIGHEST,
        preferred_element_type=jnp.float32,
    )
    mixed = jnp.dot(
        mixer,
        returned_rows.astype(jnp.float32),
        precision=lax.Precision.HIGHEST,
        preferred_element_type=jnp.float32,
    )
    return mixed.astype(jnp.bfloat16)


def iota(shape, dim):
    return lax.broadcasted_iota(jnp.int32, shape, dim)


def dot(a, b, contract=((1,), (0,))):
    return lax.dot_general(a, b, (contract, ((), ())), preferred_element_type=jnp.float32)


def slot_of_expert(ids_ref):
    picks, tok_rows = ids_ref.shape
    expert = iota((EXPERTS, tok_rows), 0).astype(jnp.float32)
    hot = ids_ref[0:1, :] == expert
    for pick in range(1, picks):
        hot = jnp.logical_or(hot, ids_ref[pick : pick + 1, :] == expert)
    earlier = iota((tok_rows, tok_rows), 0) < iota((tok_rows, tok_rows), 1)
    count = dot(hot.astype(jnp.bfloat16), earlier.astype(jnp.bfloat16))
    return jnp.where(hot, count, -1.0).astype(jnp.bfloat16)


def slot_rows_of(me, members, local_count):
    per_member = local_count * CAP
    total = members * per_member

    def parts(shape):
        row = iota(shape, 0)
        block = jnp.zeros(shape, jnp.int32)
        for edge in range(per_member, total, per_member):
            block = block + (row >= edge).astype(jnp.int32)
        inside = row - block * per_member
        which = jnp.zeros(shape, jnp.int32)
        for edge in range(CAP, per_member, CAP):
            which = which + (inside >= edge).astype(jnp.int32)
        return block, which, inside - which * CAP

    block, which, _ = parts((total, EXPERTS))
    expert = jnp.bitwise_xor(block, me) * local_count + which
    spread = (expert == iota((total, EXPERTS), 1)).astype(jnp.bfloat16)
    slot = parts((total, 1))[2]
    return spread, slot.astype(jnp.float32)


def gather_kernel(members, local_count, me_ref, ids_ref, tok_ref, *out_refs):
    spread, slot = slot_rows_of(me_ref[0], members, local_count)
    chooser = (dot(spread, slot_of_expert(ids_ref)) == slot).astype(jnp.bfloat16)
    rows = dot(chooser, tok_ref[...]).astype(jnp.bfloat16)
    per_member = local_count * CAP
    for member, out_ref in enumerate(out_refs):
        out_ref[...] = rows[member * per_member : (member + 1) * per_member]


def mixer_kernel(members, local_count, groups, me_ref, ids_ref, wts_ref, *out_refs):
    spread, slot = slot_rows_of(me_ref[0], members, local_count)
    chosen = dot(spread, slot_of_expert(ids_ref)) == slot
    picks, tok_rows = ids_ref.shape
    expert = iota((EXPERTS, tok_rows), 0).astype(jnp.float32)
    weight = jnp.zeros((EXPERTS, tok_rows), jnp.float32)
    for pick in range(picks):
        weight = jnp.where(
            ids_ref[pick : pick + 1, :] == expert, wts_ref[pick : pick + 1, :], weight
        )
    high = weight.astype(jnp.bfloat16)
    low = (weight - high.astype(jnp.float32)).astype(jnp.bfloat16)
    spread_high = jnp.where(chosen, dot(spread, high), 0.0).astype(jnp.bfloat16)
    spread_low = jnp.where(chosen, dot(spread, low), 0.0).astype(jnp.bfloat16)
    same = (iota((tok_rows, tok_rows), 0) == iota((tok_rows, tok_rows), 1)).astype(jnp.bfloat16)
    per_member = local_count * CAP
    for group, out_ref in zip(groups, out_refs):
        pieces = [
            part[m * per_member : (m + 1) * per_member]
            for part in (spread_high, spread_low)
            for m in group
        ]
        turned = dot(same, jnp.concatenate(pieces, axis=0), ((1,), (1,)))
        out_ref[...] = turned.astype(jnp.bfloat16)


def mlp_kernel(count, local_count, depth_block, hid_block, *refs):
    row_refs = refs[:count]
    gate_hbm, up_hbm, down_hbm = refs[count : count + 3]
    out_refs = refs[count + 3 : 2 * count + 3]
    gate_ref, up_ref, down_ref, held, sems = refs[2 * count + 3 :]
    per_member = row_refs[0].shape[0]
    depth, hid = gate_ref.shape
    copies = []

    def fetch(source, target, rows, block):
        started = []
        for start in range(0, rows, block):
            span = pl.ds(start, block)
            copy = pltpu.make_async_copy(source.at[span], target.at[span], sems.at[len(copies)])
            copy.start()
            copies.append(copy)
            started.append(copy)
        return started

    gate_copies = fetch(gate_hbm, gate_ref, depth, depth_block)
    up_copies = fetch(up_hbm, up_ref, depth, depth_block)
    down_copies = fetch(down_hbm, down_ref, hid, hid_block)
    for i, row_ref in enumerate(row_refs):
        held[i * per_member : (i + 1) * per_member] = row_ref[...]

    def into(started, ref):
        total = None
        for i, copy in enumerate(started):
            copy.wait()
            span = slice(i * depth_block, (i + 1) * depth_block)
            product = dot(held[:, span], ref[span])
            total = product if total is None else total + product
        return total

    gate_act = into(gate_copies, gate_ref)
    silu = gate_act / (1.0 + jnp.exp(-gate_act))
    hidden = silu * into(up_copies, up_ref)
    row = iota((per_member, hid), 0)
    column = iota((per_member, hid), 1)
    mine = None
    for which in range(local_count):
        here = jnp.logical_and(
            jnp.logical_and(row >= which * CAP, row < (which + 1) * CAP),
            jnp.logical_and(
                column >= which * (hid // local_count), column < (which + 1) * (hid // local_count)
            ),
        ).astype(jnp.float32)
        mine = here if mine is None else mine + here
    mine = jnp.concatenate([mine] * count, axis=0)
    hidden = jnp.where(mine > 0.0, hidden, 0.0).astype(jnp.bfloat16)
    total = None
    for i, copy in enumerate(down_copies):
        copy.wait()
        span = slice(i * hid_block, (i + 1) * hid_block)
        product = dot(hidden[:, span], down_ref[span])
        total = product if total is None else total + product
    for i, out_ref in enumerate(out_refs):
        out_ref[...] = total[i * per_member : (i + 1) * per_member].astype(jnp.bfloat16)


def mix_kernel(count, with_total, *refs):
    rows = jnp.concatenate([ref[...] for ref in refs[1 : 1 + count]] * 2, axis=0)
    mixed = dot(refs[0][...], rows)
    if with_total:
        mixed = mixed + refs[1 + count][...]
    refs[-1][...] = mixed.astype(refs[-1].dtype)


def whole(*_):
    return pl.BlockSpec(memory_space=VMEM)


def small(**kwargs):
    return pltpu.CompilerParams(vmem_limit_bytes=8 * 1024 * 1024, **kwargs)


def gather(me, ids, tokens, members, local_count):
    per_member = local_count * CAP
    model_width = tokens.shape[1]
    return pl.pallas_call(
        functools.partial(gather_kernel, members, local_count),
        out_shape=[jax.ShapeDtypeStruct((per_member, model_width), jnp.bfloat16)] * members,
        in_specs=[pl.BlockSpec(memory_space=pltpu.SMEM), whole(), whole()],
        out_specs=[whole()] * members,
        compiler_params=small(),
        name="gather",
    )(me, ids, tokens)


def mixer(me, ids, wts, members, local_count, groups):
    per_member = local_count * CAP
    tok_rows = ids.shape[1]
    return pl.pallas_call(
        functools.partial(mixer_kernel, members, local_count, groups),
        out_shape=[
            jax.ShapeDtypeStruct((tok_rows, 2 * len(group) * per_member), jnp.bfloat16)
            for group in groups
        ],
        in_specs=[pl.BlockSpec(memory_space=pltpu.SMEM), whole(), whole()],
        out_specs=[whole()] * len(groups),
        compiler_params=small(),
        name="mixer",
    )(me, ids, wts)


def block_of(size, wanted):
    return wanted if size % wanted == 0 else size


def mlp(rows, w_gate, w_up, w_down, local_count):
    count = len(rows)
    per_member, model_width = rows[0].shape
    hid = w_gate.shape[1]
    depth_block = block_of(model_width, 1280)
    hid_block = block_of(hid, 768)
    in_hbm = pl.BlockSpec(memory_space=pltpu.HBM)
    return pl.pallas_call(
        functools.partial(mlp_kernel, count, local_count, depth_block, hid_block),
        out_shape=[jax.ShapeDtypeStruct((per_member, model_width), jnp.bfloat16)] * count,
        in_specs=[whole()] * count + [in_hbm] * 3,
        out_specs=[whole()] * count,
        scratch_shapes=[
            VMEM((model_width, hid), jnp.bfloat16),
            VMEM((model_width, hid), jnp.bfloat16),
            VMEM((hid, model_width), jnp.bfloat16),
            VMEM((count * per_member, model_width), jnp.bfloat16),
            pltpu.SemaphoreType.DMA((2 * model_width // depth_block + hid // hid_block,)),
        ],
        cost_estimate=pl.CostEstimate(
            flops=6 * count * per_member * model_width * hid,
            bytes_accessed=6 * model_width * hid,
            transcendentals=count * per_member * hid,
        ),
        compiler_params=pltpu.CompilerParams(vmem_limit_bytes=52 * 1024 * 1024),
    )(*rows, w_gate, w_up, w_down)


def mix(shares, rows, total, dtype):
    shape = (shares.shape[0], rows[0].shape[1])
    args = [shares, *rows] + ([] if total is None else [total])
    return pl.pallas_call(
        functools.partial(mix_kernel, len(rows), total is not None),
        out_shape=jax.ShapeDtypeStruct(shape, dtype),
        in_specs=[whole()] * len(args),
        out_specs=whole(),
        compiler_params=small(),
    )(*args)


def masks_of(members):
    half = members // 2
    first = list(range(1, half // 2)) + list(range(half, half + half // 2))
    last = list(range(half // 2, half)) + list(range(half + half // 2, members))
    return first, last


def whole_experts(tokens, expert_ids, gate_weights, w_gate, w_up, w_down):
    members = lax.axis_size("expert")
    local_count = EXPERTS // members
    me = lax.axis_index("expert").astype(jnp.int32).reshape(1)
    ids, wts = expert_ids.T.astype(jnp.float32), gate_weights.T
    first, last = masks_of(members)
    early = [0] + first

    def move(value, mask):
        return lax.ppermute(value, "expert", [(i, i ^ mask) for i in range(members)])

    sent = gather(me, ids, tokens, members, local_count)
    arrived = {m: move(sent[m], m) if m else sent[0] for m in range(members)}
    shares = mixer(me, ids, wts, members, local_count, (early, last))
    back = {}
    for group in (early, last):
        done = mlp([arrived[m] for m in group], w_gate, w_up, w_down, local_count)
        for m, value in zip(group, done):
            back[m] = move(value, m) if m else value
    total = mix(shares[0], [back[m] for m in early], None, jnp.float32)
    return mix(shares[1], [back[m] for m in last], total, jnp.bfloat16)


def per_device(tokens, expert_ids, gate_weights, w_gate, w_up, w_down):
    members = lax.axis_size("expert")
    args = (tokens, expert_ids, gate_weights, w_gate, w_up, w_down)
    if members > EXPERTS:
        return split_experts(*args)
    return whole_experts(*args)


def solution(mesh):
    in_specs = (
        P(("dp", "expert"), None),
        P(("dp", "expert"), None),
        P(("dp", "expert"), None),
        P(None, "expert"),
        P(None, "expert"),
        P("expert", None),
    )
    out_specs = P(("dp", "expert"), None)
    return jax.shard_map(
        per_device, mesh=mesh, in_specs=in_specs, out_specs=out_specs, check_vma=False
    )
```

time: 115 us -> 88.5 us (0.77)
  the two profiles are of different devices: /device:TPU:0 before, /device:TPU:20 now
where the time goes in v1:
time: 88.5 us; the launch traced here: 88.3 us
  waiting for transfers between devices  45 us (51%)
  Pallas kernels  21.7 us (25%)
  starting transfers between devices  19.8 us (22%)
  local copies, waits for them, and re-layouts  1.09 us (1%)
    ppermute x14, waiting for transfers between devices, move(): lax.ppermute(value, 'expert', [(i, i ^ mask) for i in range(members)])  45 us
    ppermute x14, starting transfers between devices, move(): lax.ppermute(value, 'expert', [(i, i ^ mask) for i in range(members)])  19.8 us
    pallas_call x2, Pallas kernels, mlp(): pl.pallas_call(functools.partial(mlp_kernel, count, local_count, depth_bl...  18.6 us
    pallas_call x2, Pallas kernels, mix(): pl.pallas_call(functools.partial(mix_kernel, len(rows), total is not None...  1.84 us
  transfers between devices with their start and end apart: 14, of which 9 were waited for; matrix products, arithmetic and copies ran while one was open for 0% of the time, Pallas kernels for 22%

profile of v1, /device:TPU:20, one launch (start us, length us, event | category | flops | bytes accessed | tf_op | source)
XLA Modules:
  0.0 88.3 jit_solution(16229052858684151852)
XLA Ops:
  0.0 0.7 convert_bitcast_fusion.ids_ref
  0.7 0.0 copy-start
  0.7 1.1 %copy-done = bf16[128,2560]{1,0:T(8,128)(2,1)S(1)} copy-done((bf16[128,2560]{1,0:T(8,128)(2,1)S(1)}, bf16[128,2560]{1,0:T(8,128)(2,1)}, u32[]{:S(2)}) %copy-start) | copy-done | bytes 655384
  1.8 0.8 gather.1
  2.6 0.6 collective-permute-start.8
  3.2 0.0 collective-permute-start.9
  3.2 3.9 %collective-permute-start.10 = (bf16[40,2560]{1,0:T(8,128)(2,1)S(1)}, bf16[40,2560]{1,0:T(8,128)(2,1)S(1)}, u32[]{:S(2)}, u32[]{:S(2)}) collective-permute-start(bf16[40,2560]{1,0:T(8,128)(2,1)S(1)} %get-tuple-element.36), channel_id=1, source_target_pairs={{0,5},{1,4},{2,7},{3,6},{4,1},{5,0},{6,3},{7,2},{8,13},{9,12},{10,... | collective-permute-start | bytes 614408 | tf_op jit(solution)/shard_map/ppermute | solution.py:320
  7.0 1.6 %collective-permute-start = (bf16[40,2560]{1,0:T(8,128)(2,1)S(1)}, bf16[40,2560]{1,0:T(8,128)(2,1)S(1)}, u32[]{:S(2)}, u32[]{:S(2)}) collective-permute-start(bf16[40,2560]{1,0:T(8,128)(2,1)S(1)} %get-tuple-element.24), channel_id=1, source_target_pairs={{0,2},{1,3},{2,0},{3,1},{4,6},{5,7},{6,4},{7,5},{8,10},{9,11},{10,... | collective-permute-start | bytes 614408 | tf_op jit(solution)/shard_map/ppermute | solution.py:320
  8.6 0.4 collective-permute-start.1
  9.0 0.5 collective-permute-done.8.refs_1_
  9.5 0.4 collective-permute-start.2
  9.9 7.5 %collective-permute-done.9.refs_2_ = bf16[40,2560]{1,0:T(8,128)(2,1)S(1)} collective-permute-done((bf16[40,2560]{1,0:T(8,128)(2,1)S(1)}, bf16[40,2560]{1,0:T(8,128)(2,1)S(1)}, u32[]{:S(2)}, u32[]{:S(2)}) %collective-permute-start.9) | collective-permute-done | bytes 204832 | tf_op jit(solution)/shard_map/ppermute | solution.py:320
  17.4 2.6 %collective-permute-start.3 = (bf16[40,2560]{1,0:T(8,128)(2,1)S(1)}, bf16[40,2560]{1,0:T(8,128)(2,1)S(1)}, u32[]{:S(2)}, u32[]{:S(2)}) collective-permute-start(bf16[40,2560]{1,0:T(8,128)(2,1)S(1)} %get-tuple-element.27), channel_id=1, source_target_pairs={{0,7},{1,6},{2,5},{3,4},{4,3},{5,2},{6,1},{7,0},{8,15},{9,14},{10,... | collective-permute-start | bytes 614408 | tf_op jit(solution)/shard_map/ppermute | solution.py:320
  20.0 2.5 %collective-permute-done.10.refs_3_ = bf16[40,2560]{1,0:T(8,128)(2,1)S(1)} collective-permute-done((bf16[40,2560]{1,0:T(8,128)(2,1)S(1)}, bf16[40,2560]{1,0:T(8,128)(2,1)S(1)}, u32[]{:S(2)}, u32[]{:S(2)}) %collective-permute-start.10) | collective-permute-done | bytes 204832 | tf_op jit(solution)/shard_map/ppermute | solution.py:320
  22.6 9.3 %shard_map.65 = (bf16[40,2560]{1,0:T(8,128)(2,1)S(1)}, bf16[40,2560]{1,0:T(8,128)(2,1)S(1)}, bf16[40,2560]{1,0:T(8,128)(2,1)S(1)}, bf16[40,2560]{1,0:T(8,128)(2,1)S(1)}) custom-call(bf16[40,2560]{1,0:T(8,128)(2,1)S(1)} %get-tuple-element.33.refs_0_, bf16[40,2560]{1,0:T(8,128)(2,1)S(1)} %collective-permute-done.8.refs_1_, ...), custom_call_target="tpu_custom_call" | custom-call | flops 3774873600 | bytes 23592960 | tf_op jit(solution)/shard_map/pallas_call | solution.py:271
  31.8 1.9 %collective-permute-start.11 = (bf16[40,2560]{1,0:T(8,128)(2,1)S(1)}, bf16[40,2560]{1,0:T(8,128)(2,1)S(1)}, u32[]{:S(2)}, u32[]{:S(2)}) collective-permute-start(bf16[40,2560]{1,0:T(8,128)(2,1)S(1)} %get-tuple-element.38), channel_id=1, source_target_pairs={{0,1},{1,0},{2,3},{3,2},{4,5},{5,4},{6,7},{7,6},{8,9},{9,8},{10,11... | collective-permute-start | bytes 614408 | tf_op jit(solution)/shard_map/ppermute | solution.py:320
  33.7 0.0 collective-permute-done.refs_0_
  33.7 0.0 copy-start.1
  33.7 3.5 %collective-permute-start.12 = (bf16[40,2560]{1,0:T(8,128)(2,1)S(1)}, bf16[40,2560]{1,0:T(8,128)(2,1)S(1)}, u32[]{:S(2)}, u32[]{:S(2)}) collective-permute-start(bf16[40,2560]{1,0:T(8,128)(2,1)S(1)} %get-tuple-element.39), channel_id=1, source_target_pairs={{0,4},{1,5},{2,6},{3,7},{4,0},{5,1},{6,2},{7,3},{8,12},{9,13},{10,... | collective-permute-start | bytes 614408 | tf_op jit(solution)/shard_map/ppermute | solution.py:320
  37.2 0.0 collective-permute-done.1.refs_1_
  37.2 4.2 %collective-permute-done.2.refs_2_ = bf16[40,2560]{1,0:T(8,128)(2,1)S(1)} collective-permute-done((bf16[40,2560]{1,0:T(8,128)(2,1)S(1)}, bf16[40,2560]{1,0:T(8,128)(2,1)S(1)}, u32[]{:S(2)}, u32[]{:S(2)}) %collective-permute-start.2) | collective-permute-done | bytes 204832 | tf_op jit(solution)/shard_map/ppermute | solution.py:320
  41.5 5.3 %collective-permute-done.3.refs_3_ = bf16[40,2560]{1,0:T(8,128)(2,1)S(1)} collective-permute-done((bf16[40,2560]{1,0:T(8,128)(2,1)S(1)}, bf16[40,2560]{1,0:T(8,128)(2,1)S(1)}, u32[]{:S(2)}, u32[]{:S(2)}) %collective-permute-start.3) | collective-permute-done | bytes 204832 | tf_op jit(solution)/shard_map/ppermute | solution.py:320
  46.8 9.3 %shard_map.64 = (bf16[40,2560]{1,0:T(8,128)(2,1)S(1)}, bf16[40,2560]{1,0:T(8,128)(2,1)S(1)}, bf16[40,2560]{1,0:T(8,128)(2,1)S(1)}, bf16[40,2560]{1,0:T(8,128)(2,1)S(1)}) custom-call(bf16[40,2560]{1,0:T(8,128)(2,1)S(1)} %collective-permute-done.refs_0_, bf16[40,2560]{1,0:T(8,128)(2,1)S(1)} %collective-permute-done.1.refs_1_, ...), custom_call_target="tpu_custom_call" | custom-call | flops 3774873600 | bytes 23592960 | tf_op jit(solution)/shard_map/pallas_call | solution.py:271
  56.1 0.1 collective-permute-start.4
  56.2 1.8 %collective-permute-start.13 = (bf16[40,2560]{1,0:T(8,128)(2,1)S(1)}, bf16[40,2560]{1,0:T(8,128)(2,1)S(1)}, u32[]{:S(2)}, u32[]{:S(2)}) collective-permute-start(bf16[40,2560]{1,0:T(8,128)(2,1)S(1)} %get-tuple-element.40), channel_id=1, source_target_pairs={{0,5},{1,4},{2,7},{3,6},{4,1},{5,0},{6,3},{7,2},{8,13},{9,12},{10,... | collective-permute-start | bytes 614408 | tf_op jit(solution)/shard_map/ppermute | solution.py:320
  58.0 1.1 %collective-permute-start.5 = (bf16[40,2560]{1,0:T(8,128)(2,1)S(1)}, bf16[40,2560]{1,0:T(8,128)(2,1)S(1)}, u32[]{:S(2)}, u32[]{:S(2)}) collective-permute-start(bf16[40,2560]{1,0:T(8,128)(2,1)S(1)} %get-tuple-element.29), channel_id=1, source_target_pairs={{0,3},{1,2},{2,1},{3,0},{4,7},{5,6},{6,5},{7,4},{8,11},{9,10},{10,... | collective-permute-start | bytes 614408 | tf_op jit(solution)/shard_map/ppermute | solution.py:320
  59.1 0.0 collective-permute-done.11.refs_2_
  59.1 1.5 %collective-permute-start.6 = (bf16[40,2560]{1,0:T(8,128)(2,1)S(1)}, bf16[40,2560]{1,0:T(8,128)(2,1)S(1)}, u32[]{:S(2)}, u32[]{:S(2)}) collective-permute-start(bf16[40,2560]{1,0:T(8,128)(2,1)S(1)} %get-tuple-element.30), channel_id=1, source_target_pairs={{0,6},{1,7},{2,4},{3,5},{4,2},{5,3},{6,0},{7,1},{8,14},{9,15},{10,... | collective-permute-start | bytes 614408 | tf_op jit(solution)/shard_map/ppermute | solution.py:320
  60.6 0.0 collective-permute-done.12.refs_3_
  60.6 0.5 collective-permute-start.7
  61.1 0.0 copy-done.1
  61.1 0.5 mixer.1
  61.6 6.3 %collective-permute-done.13.refs_4_ = bf16[40,2560]{1,0:T(8,128)(2,1)S(1)} collective-permute-done((bf16[40,2560]{1,0:T(8,128)(2,1)S(1)}, bf16[40,2560]{1,0:T(8,128)(2,1)S(1)}, u32[]{:S(2)}, u32[]{:S(2)}) %collective-permute-start.13) | collective-permute-done | bytes 204832 | tf_op jit(solution)/shard_map/ppermute | solution.py:320
  68.0 0.5 shard_map.66.refs_5_
  68.5 0.0 collective-permute-done.4.refs_1_
  68.5 4.5 %collective-permute-done.5.refs_2_ = bf16[40,2560]{1,0:T(8,128)(2,1)S(1)} collective-permute-done((bf16[40,2560]{1,0:T(8,128)(2,1)S(1)}, bf16[40,2560]{1,0:T(8,128)(2,1)S(1)}, u32[]{:S(2)}, u32[]{:S(2)}) %collective-permute-start.5) | collective-permute-done | bytes 204832 | tf_op jit(solution)/shard_map/ppermute | solution.py:320
  73.0 9.3 %collective-permute-done.6.refs_3_ = bf16[40,2560]{1,0:T(8,128)(2,1)S(1)} collective-permute-done((bf16[40,2560]{1,0:T(8,128)(2,1)S(1)}, bf16[40,2560]{1,0:T(8,128)(2,1)S(1)}, u32[]{:S(2)}, u32[]{:S(2)}) %collective-permute-start.6) | collective-permute-done | bytes 204832 | tf_op jit(solution)/shard_map/ppermute | solution.py:320
  82.3 4.7 %collective-permute-done.7.refs_4_ = bf16[40,2560]{1,0:T(8,128)(2,1)S(1)} collective-permute-done((bf16[40,2560]{1,0:T(8,128)(2,1)S(1)}, bf16[40,2560]{1,0:T(8,128)(2,1)S(1)}, u32[]{:S(2)}, u32[]{:S(2)}) %collective-permute-start.7) | collective-permute-done | bytes 204832 | tf_op jit(solution)/shard_map/ppermute | solution.py:320
  87.0 1.4 %shard_map.67 = bf16[128,2560]{1,0:T(8,128)(2,1)} custom-call(bf16[128,320]{1,0:T(8,128)(2,1)S(1)} %get-tuple-element.23.refs_0_, bf16[40,2560]{1,0:T(8,128)(2,1)S(1)} %collective-permute-done.4.refs_1_, bf16[40,2560]{1,0:T(8,128)(2,1)S(1)} %collective-permute-done.5.refs_2_, bf16[40,2560]{1,0:T(8,128)(2,1)S(1)} %collective-permute-done.6.refs_3_, ...), custom_call_target="tpu_custom_call" | custom-call | tf_op jit(solution)/shard_map/pallas_call | solution.py:295
Async XLA Ops:
  0.7 1.1 %copy-start = (bf16[128,2560]{1,0:T(8,128)(2,1)S(1)}, bf16[128,2560]{1,0:T(8,128)(2,1)}, u32[]{:S(2)}) copy-start(bf16[128,2560]{1,0:T(8,128)(2,1)} %tok_ref.1) | copy-start | bytes 1966084
  2.6 6.9 %collective-permute-start.8 = (bf16[40,2560]{1,0:T(8,128)(2,1)S(1)}, bf16[40,2560]{1,0:T(8,128)(2,1)S(1)}, u32[]{:S(2)}, u32[]{:S(2)}) collective-permute-start(bf16[40,2560]{1,0:T(8,128)(2,1)S(1)} %get-tuple-element.34), channel_id=1, source_target_pairs={{0,1},{1,0},{2,3},{3,2},{4,5},{5,4},{6,7},{7,6},{8,9},{9,8},{10,11... | collective-permute-start | bytes 614408 | tf_op jit(solution)/shard_map/ppermute | solution.py:320
  3.2 14.3 %collective-permute-start.9 = (bf16[40,2560]{1,0:T(8,128)(2,1)S(1)}, bf16[40,2560]{1,0:T(8,128)(2,1)S(1)}, u32[]{:S(2)}, u32[]{:S(2)}) collective-permute-start(bf16[40,2560]{1,0:T(8,128)(2,1)S(1)} %get-tuple-element.35), channel_id=1, source_target_pairs={{0,4},{1,5},{2,6},{3,7},{4,0},{5,1},{6,2},{7,3},{8,12},{9,13},{10,... | collective-permute-start | bytes 614408 | tf_op jit(solution)/shard_map/ppermute | solution.py:320
  3.2 19.4 %collective-permute-start.10 = (bf16[40,2560]{1,0:T(8,128)(2,1)S(1)}, bf16[40,2560]{1,0:T(8,128)(2,1)S(1)}, u32[]{:S(2)}, u32[]{:S(2)}) collective-permute-start(bf16[40,2560]{1,0:T(8,128)(2,1)S(1)} %get-tuple-element.36), channel_id=1, source_target_pairs={{0,5},{1,4},{2,7},{3,6},{4,1},{5,0},{6,3},{7,2},{8,13},{9,12},{10,... | collective-permute-start | bytes 614408 | tf_op jit(solution)/shard_map/ppermute | solution.py:320
  7.0 26.7 %collective-permute-start = (bf16[40,2560]{1,0:T(8,128)(2,1)S(1)}, bf16[40,2560]{1,0:T(8,128)(2,1)S(1)}, u32[]{:S(2)}, u32[]{:S(2)}) collective-permute-start(bf16[40,2560]{1,0:T(8,128)(2,1)S(1)} %get-tuple-element.24), channel_id=1, source_target_pairs={{0,2},{1,3},{2,0},{3,1},{4,6},{5,7},{6,4},{7,5},{8,10},{9,11},{10,... | collective-permute-start | bytes 614408 | tf_op jit(solution)/shard_map/ppermute | solution.py:320
  8.6 28.6 %collective-permute-start.1 = (bf16[40,2560]{1,0:T(8,128)(2,1)S(1)}, bf16[40,2560]{1,0:T(8,128)(2,1)S(1)}, u32[]{:S(2)}, u32[]{:S(2)}) collective-permute-start(bf16[40,2560]{1,0:T(8,128)(2,1)S(1)} %get-tuple-element.25), channel_id=1, source_target_pairs={{0,3},{1,2},{2,1},{3,0},{4,7},{5,6},{6,5},{7,4},{8,11},{9,10},{10,... | collective-permute-start | bytes 614408 | tf_op jit(solution)/shard_map/ppermute | solution.py:320
  9.5 32.0 %collective-permute-start.2 = (bf16[40,2560]{1,0:T(8,128)(2,1)S(1)}, bf16[40,2560]{1,0:T(8,128)(2,1)S(1)}, u32[]{:S(2)}, u32[]{:S(2)}) collective-permute-start(bf16[40,2560]{1,0:T(8,128)(2,1)S(1)} %get-tuple-element.26), channel_id=1, source_target_pairs={{0,6},{1,7},{2,4},{3,5},{4,2},{5,3},{6,0},{7,1},{8,14},{9,15},{10,... | collective-permute-start | bytes 614408 | tf_op jit(solution)/shard_map/ppermute | solution.py:320
  17.4 29.4 %collective-permute-start.3 = (bf16[40,2560]{1,0:T(8,128)(2,1)S(1)}, bf16[40,2560]{1,0:T(8,128)(2,1)S(1)}, u32[]{:S(2)}, u32[]{:S(2)}) collective-permute-start(bf16[40,2560]{1,0:T(8,128)(2,1)S(1)} %get-tuple-element.27), channel_id=1, source_target_pairs={{0,7},{1,6},{2,5},{3,4},{4,3},{5,2},{6,1},{7,0},{8,15},{9,14},{10,... | collective-permute-start | bytes 614408 | tf_op jit(solution)/shard_map/ppermute | solution.py:320
  31.8 27.3 %collective-permute-start.11 = (bf16[40,2560]{1,0:T(8,128)(2,1)S(1)}, bf16[40,2560]{1,0:T(8,128)(2,1)S(1)}, u32[]{:S(2)}, u32[]{:S(2)}) collective-permute-start(bf16[40,2560]{1,0:T(8,128)(2,1)S(1)} %get-tuple-element.38), channel_id=1, source_target_pairs={{0,1},{1,0},{2,3},{3,2},{4,5},{5,4},{6,7},{7,6},{8,9},{9,8},{10,11... | collective-permute-start | bytes 614408 | tf_op jit(solution)/shard_map/ppermute | solution.py:320
  33.7 27.4 %copy-start.1 = (f32[128,2]{0,1:T(2,128)S(1)}, f32[128,2]{0,1:T(2,128)}, u32[]{:S(2)}) copy-start(f32[128,2]{0,1:T(2,128)} %param.8) | copy-start | bytes 3076
  33.7 26.9 %collective-permute-start.12 = (bf16[40,2560]{1,0:T(8,128)(2,1)S(1)}, bf16[40,2560]{1,0:T(8,128)(2,1)S(1)}, u32[]{:S(2)}, u32[]{:S(2)}) collective-permute-start(bf16[40,2560]{1,0:T(8,128)(2,1)S(1)} %get-tuple-element.39), channel_id=1, source_target_pairs={{0,4},{1,5},{2,6},{3,7},{4,0},{5,1},{6,2},{7,3},{8,12},{9,13},{10,... | collective-permute-start | bytes 614408 | tf_op jit(solution)/shard_map/ppermute | solution.py:320
  56.1 12.4 %collective-permute-start.4 = (bf16[40,2560]{1,0:T(8,128)(2,1)S(1)}, bf16[40,2560]{1,0:T(8,128)(2,1)S(1)}, u32[]{:S(2)}, u32[]{:S(2)}) collective-permute-start(bf16[40,2560]{1,0:T(8,128)(2,1)S(1)} %get-tuple-element.28), channel_id=1, source_target_pairs={{0,2},{1,3},{2,0},{3,1},{4,6},{5,7},{6,4},{7,5},{8,10},{9,11},{10,... | collective-permute-start | bytes 614408 | tf_op jit(solution)/shard_map/ppermute | solution.py:320
  56.2 11.8 %collective-permute-start.13 = (bf16[40,2560]{1,0:T(8,128)(2,1)S(1)}, bf16[40,2560]{1,0:T(8,128)(2,1)S(1)}, u32[]{:S(2)}, u32[]{:S(2)}) collective-permute-start(bf16[40,2560]{1,0:T(8,128)(2,1)S(1)} %get-tuple-element.40), channel_id=1, source_target_pairs={{0,5},{1,4},{2,7},{3,6},{4,1},{5,0},{6,3},{7,2},{8,13},{9,12},{10,... | collective-permute-start | bytes 614408 | tf_op jit(solution)/shard_map/ppermute | solution.py:320
  58.0 15.0 %collective-permute-start.5 = (bf16[40,2560]{1,0:T(8,128)(2,1)S(1)}, bf16[40,2560]{1,0:T(8,128)(2,1)S(1)}, u32[]{:S(2)}, u32[]{:S(2)}) collective-permute-start(bf16[40,2560]{1,0:T(8,128)(2,1)S(1)} %get-tuple-element.29), channel_id=1, source_target_pairs={{0,3},{1,2},{2,1},{3,0},{4,7},{5,6},{6,5},{7,4},{8,11},{9,10},{10,... | collective-permute-start | bytes 614408 | tf_op jit(solution)/shard_map/ppermute | solution.py:320
  59.1 23.2 %collective-permute-start.6 = (bf16[40,2560]{1,0:T(8,128)(2,1)S(1)}, bf16[40,2560]{1,0:T(8,128)(2,1)S(1)}, u32[]{:S(2)}, u32[]{:S(2)}) collective-permute-start(bf16[40,2560]{1,0:T(8,128)(2,1)S(1)} %get-tuple-element.30), channel_id=1, source_target_pairs={{0,6},{1,7},{2,4},{3,5},{4,2},{5,3},{6,0},{7,1},{8,14},{9,15},{10,... | collective-permute-start | bytes 614408 | tf_op jit(solution)/shard_map/ppermute | solution.py:320
  60.6 26.4 %collective-permute-start.7 = (bf16[40,2560]{1,0:T(8,128)(2,1)S(1)}, bf16[40,2560]{1,0:T(8,128)(2,1)S(1)}, u32[]{:S(2)}, u32[]{:S(2)}) collective-permute-start(bf16[40,2560]{1,0:T(8,128)(2,1)S(1)} %get-tuple-element.31), channel_id=1, source_target_pairs={{0,7},{1,6},{2,5},{3,4},{4,3},{5,2},{6,1},{7,0},{8,15},{9,14},{10,... | collective-permute-start | bytes 614408 | tf_op jit(solution)/shard_map/ppermute | solution.py:320

commit v2 on v1

--- a/solution.py
+++ b/solution.py
@@ -86,7 +86,7 @@
 
 def slot_of_expert(ids_ref):
     picks, tok_rows = ids_ref.shape
-    expert = iota((EXPERTS, tok_rows), 0).astype(jnp.float32)
+    expert = iota((EXPERTS, tok_rows), 0)
     hot = ids_ref[0:1, :] == expert
     for pick in range(1, picks):
         hot = jnp.logical_or(hot, ids_ref[pick : pick + 1, :] == expert)
@@ -117,9 +117,17 @@
     return spread, slot.astype(jnp.float32)
 
 
-def gather_kernel(members, local_count, me_ref, ids_ref, tok_ref, *out_refs):
+def gather_kernel(members, local_count, me_ref, ids_hbm, tok_hbm, *refs):
+    out_refs = refs[:members]
+    ids_ref, tok_ref, sems = refs[members:]
+    ids_copy = pltpu.make_async_copy(ids_hbm, ids_ref, sems.at[0])
+    tok_copy = pltpu.make_async_copy(tok_hbm, tok_ref, sems.at[1])
+    ids_copy.start()
+    tok_copy.start()
     spread, slot = slot_rows_of(me_ref[0], members, local_count)
+    ids_copy.wait()
     chooser = (dot(spread, slot_of_expert(ids_ref)) == slot).astype(jnp.bfloat16)
+    tok_copy.wait()
     rows = dot(chooser, tok_ref[...]).astype(jnp.bfloat16)
     per_member = local_count * CAP
     for member, out_ref in enumerate(out_refs):
@@ -130,7 +138,7 @@
     spread, slot = slot_rows_of(me_ref[0], members, local_count)
     chosen = dot(spread, slot_of_expert(ids_ref)) == slot
     picks, tok_rows = ids_ref.shape
-    expert = iota((EXPERTS, tok_rows), 0).astype(jnp.float32)
+    expert = iota((EXPERTS, tok_rows), 0)
     weight = jnp.zeros((EXPERTS, tok_rows), jnp.float32)
     for pick in range(picks):
         weight = jnp.where(
@@ -224,6 +232,10 @@
     return pl.BlockSpec(memory_space=VMEM)
 
 
+def in_hbm(value):
+    return pltpu.with_memory_space_constraint(value, pltpu.HBM)
+
+
 def small(**kwargs):
     return pltpu.CompilerParams(vmem_limit_bytes=8 * 1024 * 1024, **kwargs)
 
@@ -234,11 +246,16 @@
     return pl.pallas_call(
         functools.partial(gather_kernel, members, local_count),
         out_shape=[jax.ShapeDtypeStruct((per_member, model_width), jnp.bfloat16)] * members,
-        in_specs=[pl.BlockSpec(memory_space=pltpu.SMEM), whole(), whole()],
+        in_specs=[pl.BlockSpec(memory_space=pltpu.SMEM)] + [pl.BlockSpec(memory_space=pltpu.HBM)] * 2,
         out_specs=[whole()] * members,
+        scratch_shapes=[
+            VMEM(ids.shape, ids.dtype),
+            VMEM(tokens.shape, tokens.dtype),
+            pltpu.SemaphoreType.DMA((2,)),
+        ],
         compiler_params=small(),
         name="gather",
-    )(me, ids, tokens)
+    )(me, in_hbm(ids), in_hbm(tokens))
 
 
 def mixer(me, ids, wts, members, local_count, groups):
@@ -267,11 +284,10 @@
     hid = w_gate.shape[1]
     depth_block = block_of(model_width, 1280)
     hid_block = block_of(hid, 768)
-    in_hbm = pl.BlockSpec(memory_space=pltpu.HBM)
     return pl.pallas_call(
         functools.partial(mlp_kernel, count, local_count, depth_block, hid_block),
         out_shape=[jax.ShapeDtypeStruct((per_member, model_width), jnp.bfloat16)] * count,
-        in_specs=[whole()] * count + [in_hbm] * 3,
+        in_specs=[whole()] * count + [pl.BlockSpec(memory_space=pltpu.HBM)] * 3,
         out_specs=[whole()] * count,
         scratch_shapes=[
             VMEM((model_width, hid), jnp.bfloat16),
@@ -285,8 +301,8 @@
             bytes_accessed=6 * model_width * hid,
             transcendentals=count * per_member * hid,
         ),
-        compiler_params=pltpu.CompilerParams(vmem_limit_bytes=52 * 1024 * 1024),
-    )(*rows, w_gate, w_up, w_down)
+        compiler_params=pltpu.CompilerParams(vmem_limit_bytes=40 * 1024 * 1024),
+    )(*rows, in_hbm(w_gate), in_hbm(w_up), in_hbm(w_down))
 
 
 def mix(shares, rows, total, dtype):
@@ -303,16 +319,15 @@
 
 def masks_of(members):
     half = members // 2
-    first = list(range(1, half // 2)) + list(range(half, half + half // 2))
-    last = list(range(half // 2, half)) + list(range(half + half // 2, members))
-    return first, last
+    far = list(range(half, members))
+    return list(range(1, half)) + far[: half // 2], far[half // 2 :]
 
 
 def whole_experts(tokens, expert_ids, gate_weights, w_gate, w_up, w_down):
     members = lax.axis_size("expert")
     local_count = EXPERTS // members
     me = lax.axis_index("expert").astype(jnp.int32).reshape(1)
-    ids, wts = expert_ids.T.astype(jnp.float32), gate_weights.T
+    ids, wts = expert_ids.T, gate_weights.T
     first, last = masks_of(members)
     early = [0] + first
 

time: 88.5 us -> 86.1 us (0.973)
  the two profiles are of different devices: /device:TPU:20 before, /device:TPU:22 now
where the time goes in v2:
time: 86.1 us; the launch traced here: 86 us
  waiting for transfers between devices  40.5 us (47%)
  Pallas kernels  23.4 us (27%)
  starting transfers between devices  22 us (26%)
    ppermute x14, waiting for transfers between devices, move(): lax.ppermute(value, 'expert', [(i, i ^ mask) for i in range(members)])  40.5 us
    ppermute x14, starting transfers between devices, move(): lax.ppermute(value, 'expert', [(i, i ^ mask) for i in range(members)])  22 us
    pallas_call x2, Pallas kernels, mlp(): pl.pallas_call(functools.partial(mlp_kernel, count, local_count, depth_bl...  19.5 us
  transfers between devices with their start and end apart: 14, of which 7 were waited for; matrix products, arithmetic and copies ran while one was open for 0% of the time, Pallas kernels for 24%

profile of v2, /device:TPU:22, one launch (start us, length us, event | category | flops | bytes accessed | tf_op | source)
XLA Modules:
  0.0 86.0 jit_solution(9206286173527617287)
XLA Ops:
  0.0 1.7 %gather.1 = (bf16[40,2560]{1,0:T(8,128)(2,1)S(1)}, bf16[40,2560]{1,0:T(8,128)(2,1)S(1)}, bf16[40,2560]{1,0:T(8,128)(2,1)S(1)}, bf16[40,2560]{1,0:T(8,128)(2,1)S(...) custom-call(s32[1]{0:T(128)} %bitcast.me_ref, ...), custom_call_target="tpu_custom_call" | custom-call | tf_op jit(solution)/shard_map/gather/pallas_call | solution.py:246
  1.7 0.6 collective-permute-start.4
  2.3 1.6 %collective-permute-start.5 = (bf16[40,2560]{1,0:T(8,128)(2,1)S(1)}, bf16[40,2560]{1,0:T(8,128)(2,1)S(1)}, u32[]{:S(2)}, u32[]{:S(2)}) collective-permute-start(bf16[40,2560]{1,0:T(8,128)(2,1)S(1)} %get-tuple-element.31), channel_id=1, source_target_pairs={{0,2},{1,3},{2,0},{3,1},{4,6},{5,7},{6,4},{7,5},{8,10},{9,11},{10,... | collective-permute-start | bytes 614408 | tf_op jit(solution)/shard_map/ppermute | solution.py:335
  3.9 1.4 %collective-permute-start.6 = (bf16[40,2560]{1,0:T(8,128)(2,1)S(1)}, bf16[40,2560]{1,0:T(8,128)(2,1)S(1)}, u32[]{:S(2)}, u32[]{:S(2)}) collective-permute-start(bf16[40,2560]{1,0:T(8,128)(2,1)S(1)} %get-tuple-element.32), channel_id=1, source_target_pairs={{0,3},{1,2},{2,1},{3,0},{4,7},{5,6},{6,5},{7,4},{8,11},{9,10},{10,... | collective-permute-start | bytes 614408 | tf_op jit(solution)/shard_map/ppermute | solution.py:335
  5.3 0.3 collective-permute-start.7
  5.6 2.5 %collective-permute-start.8 = (bf16[40,2560]{1,0:T(8,128)(2,1)S(1)}, bf16[40,2560]{1,0:T(8,128)(2,1)S(1)}, u32[]{:S(2)}, u32[]{:S(2)}) collective-permute-start(bf16[40,2560]{1,0:T(8,128)(2,1)S(1)} %get-tuple-element.34), channel_id=1, source_target_pairs={{0,5},{1,4},{2,7},{3,6},{4,1},{5,0},{6,3},{7,2},{8,13},{9,12},{10,... | collective-permute-start | bytes 614408 | tf_op jit(solution)/shard_map/ppermute | solution.py:335
  8.1 0.7 collective-permute-done.4.refs_1_
  8.8 0.5 collective-permute-start
  9.3 5.3 %collective-permute-done.5.refs_2_ = bf16[40,2560]{1,0:T(8,128)(2,1)S(1)} collective-permute-done((bf16[40,2560]{1,0:T(8,128)(2,1)S(1)}, bf16[40,2560]{1,0:T(8,128)(2,1)S(1)}, u32[]{:S(2)}, u32[]{:S(2)}) %collective-permute-start.5) | collective-permute-done | bytes 204832 | tf_op jit(solution)/shard_map/ppermute | solution.py:335
  14.6 3.1 %collective-permute-start.1 = (bf16[40,2560]{1,0:T(8,128)(2,1)S(1)}, bf16[40,2560]{1,0:T(8,128)(2,1)S(1)}, u32[]{:S(2)}, u32[]{:S(2)}) collective-permute-start(bf16[40,2560]{1,0:T(8,128)(2,1)S(1)} %get-tuple-element.25), channel_id=1, source_target_pairs={{0,7},{1,6},{2,5},{3,4},{4,3},{5,2},{6,1},{7,0},{8,15},{9,14},{10,... | collective-permute-start | bytes 614408 | tf_op jit(solution)/shard_map/ppermute | solution.py:335
  17.7 0.0 collective-permute-done.6.refs_3_
  17.7 1.3 %collective-permute-done.7.refs_4_ = bf16[40,2560]{1,0:T(8,128)(2,1)S(1)} collective-permute-done((bf16[40,2560]{1,0:T(8,128)(2,1)S(1)}, bf16[40,2560]{1,0:T(8,128)(2,1)S(1)}, u32[]{:S(2)}, u32[]{:S(2)}) %collective-permute-start.7) | collective-permute-done | bytes 204832 | tf_op jit(solution)/shard_map/ppermute | solution.py:335
  19.0 14.0 %collective-permute-done.8.refs_5_ = bf16[40,2560]{1,0:T(8,128)(2,1)S(1)} collective-permute-done((bf16[40,2560]{1,0:T(8,128)(2,1)S(1)}, bf16[40,2560]{1,0:T(8,128)(2,1)S(1)}, u32[]{:S(2)}, u32[]{:S(2)}) %collective-permute-start.8) | collective-permute-done | bytes 204832 | tf_op jit(solution)/shard_map/ppermute | solution.py:335
  33.0 10.2 %shard_map.65 = (bf16[40,2560]{1,0:T(8,128)(2,1)S(1)}, bf16[40,2560]{1,0:T(8,128)(2,1)S(1)}, bf16[40,2560]{1,0:T(8,128)(2,1)S(1)}, bf16[40,2560]{1,0:T(8,128)(2,...) custom-call(bf16[40,2560]{1,0:T(8,128)(2,1)S(1)} %get-tuple-element.29.refs_0_, ...), custom_call_target="tpu_custom_call" | custom-call | flops 5662310400 | bytes 23592960 | tf_op jit(solution)/shard_map/pallas_call | solution.py:287
  43.2 0.1 collective-permute-start.9
  43.3 6.1 %collective-permute-start.10 = (bf16[40,2560]{1,0:T(8,128)(2,1)S(1)}, bf16[40,2560]{1,0:T(8,128)(2,1)S(1)}, u32[]{:S(2)}, u32[]{:S(2)}) collective-permute-start(bf16[40,2560]{1,0:T(8,128)(2,1)S(1)} %get-tuple-element.37), channel_id=1, source_target_pairs={{0,2},{1,3},{2,0},{3,1},{4,6},{5,7},{6,4},{7,5},{8,10},{9,11},{10,... | collective-permute-start | bytes 614408 | tf_op jit(solution)/shard_map/ppermute | solution.py:335
  49.3 0.0 collective-permute-start.11
  49.3 0.0 collective-permute-done.refs_0_
  49.3 0.3 collective-permute-start.12
  49.6 0.0 collective-permute-done.1.refs_1_
  49.6 0.0 copy-start
  49.6 0.0 copy-start.1
  49.6 3.5 %collective-permute-start.13 = (bf16[40,2560]{1,0:T(8,128)(2,1)S(1)}, bf16[40,2560]{1,0:T(8,128)(2,1)S(1)}, u32[]{:S(2)}, u32[]{:S(2)}) collective-permute-start(bf16[40,2560]{1,0:T(8,128)(2,1)S(1)} %get-tuple-element.40), channel_id=1, source_target_pairs={{0,5},{1,4},{2,7},{3,6},{4,1},{5,0},{6,3},{7,2},{8,13},{9,12},{10,... | collective-permute-start | bytes 614408 | tf_op jit(solution)/shard_map/ppermute | solution.py:335
  53.2 9.3 %shard_map.64 = (bf16[40,2560]{1,0:T(8,128)(2,1)S(1)}, bf16[40,2560]{1,0:T(8,128)(2,1)S(1)}) custom-call(bf16[40,2560]{1,0:T(8,128)(2,1)S(1)} %collective-permute-done.refs_0_, bf16[40,2560]{1,0:T(8,128)(2,1)S(1)} %collective-permute-done.1.refs_1_, bf16[2560,1536]{1,0:T(8,128)(2,1)} %refs_6_.1, bf16[2560,1536]{1,0:T(8,128)(2,1)} %refs_7_.1, ...), custom_call_target="tpu_custom_call" | custom-call | flops 1887436800 | bytes 23592960 | tf_op jit(solution)/shard_map/pallas_call | solution.py:287
  62.5 0.0 collective-permute-done.9.refs_2_
  62.5 0.7 collective-permute-start.2
  63.2 0.0 collective-permute-done.10.refs_3_
  63.2 1.4 %collective-permute-start.3 = (bf16[40,2560]{1,0:T(8,128)(2,1)S(1)}, bf16[40,2560]{1,0:T(8,128)(2,1)S(1)}, u32[]{:S(2)}, u32[]{:S(2)}) collective-permute-start(bf16[40,2560]{1,0:T(8,128)(2,1)S(1)} %get-tuple-element.27), channel_id=1, source_target_pairs={{0,7},{1,6},{2,5},{3,4},{4,3},{5,2},{6,1},{7,0},{8,15},{9,14},{10,... | collective-permute-start | bytes 614408 | tf_op jit(solution)/shard_map/ppermute | solution.py:335
  64.6 0.0 copy-done
  64.6 0.0 copy-done.1
  64.6 0.5 mixer.1
  65.1 0.0 collective-permute-done.11.refs_4_
  65.1 0.0 collective-permute-done.12.refs_5_
  65.2 9.0 %collective-permute-done.13.refs_6_ = bf16[40,2560]{1,0:T(8,128)(2,1)S(1)} collective-permute-done((bf16[40,2560]{1,0:T(8,128)(2,1)S(1)}, bf16[40,2560]{1,0:T(8,128)(2,1)S(1)}, u32[]{:S(2)}, u32[]{:S(2)}) %collective-permute-start.13) | collective-permute-done | bytes 204832 | tf_op jit(solution)/shard_map/ppermute | solution.py:335
  74.2 0.5 shard_map.66.refs_3_
  74.7 6.9 %collective-permute-done.2.refs_1_ = bf16[40,2560]{1,0:T(8,128)(2,1)S(1)} collective-permute-done((bf16[40,2560]{1,0:T(8,128)(2,1)S(1)}, bf16[40,2560]{1,0:T(8,128)(2,1)S(1)}, u32[]{:S(2)}, u32[]{:S(2)}) %collective-permute-start.2) | collective-permute-done | bytes 204832 | tf_op jit(solution)/shard_map/ppermute | solution.py:335
  81.6 3.2 %collective-permute-done.3.refs_2_ = bf16[40,2560]{1,0:T(8,128)(2,1)S(1)} collective-permute-done((bf16[40,2560]{1,0:T(8,128)(2,1)S(1)}, bf16[40,2560]{1,0:T(8,128)(2,1)S(1)}, u32[]{:S(2)}, u32[]{:S(2)}) %collective-permute-start.3) | collective-permute-done | bytes 204832 | tf_op jit(solution)/shard_map/ppermute | solution.py:335
  84.8 1.2 %shard_map.67 = bf16[128,2560]{1,0:T(8,128)(2,1)} custom-call(bf16[128,160]{1,0:T(8,128)(2,1)S(1)} %get-tuple-element.23.refs_0_, bf16[40,2560]{1,0:T(8,128)(2,1)S(1)} %collective-permute-done.2.refs_1_, bf16[40,2560]{1,0:T(8,128)(2,1)S(1)} %collective-permute-done.3.refs_2_, f32[128,2560]{1,0:T(8,128)S(1)} %shard_map.66.refs_3_), custom_call_target="tpu_custom_call" | custom-call | tf_op jit(solution)/shard_map/pallas_call | solution.py:311
Async XLA Ops:
  1.7 7.1 %collective-permute-start.4 = (bf16[40,2560]{1,0:T(8,128)(2,1)S(1)}, bf16[40,2560]{1,0:T(8,128)(2,1)S(1)}, u32[]{:S(2)}, u32[]{:S(2)}) collective-permute-start(bf16[40,2560]{1,0:T(8,128)(2,1)S(1)} %get-tuple-element.30), channel_id=1, source_target_pairs={{0,1},{1,0},{2,3},{3,2},{4,5},{5,4},{6,7},{7,6},{8,9},{9,8},{10,11... | collective-permute-start | bytes 614408 | tf_op jit(solution)/shard_map/ppermute | solution.py:335
  2.3 12.3 %collective-permute-start.5 = (bf16[40,2560]{1,0:T(8,128)(2,1)S(1)}, bf16[40,2560]{1,0:T(8,128)(2,1)S(1)}, u32[]{:S(2)}, u32[]{:S(2)}) collective-permute-start(bf16[40,2560]{1,0:T(8,128)(2,1)S(1)} %get-tuple-element.31), channel_id=1, source_target_pairs={{0,2},{1,3},{2,0},{3,1},{4,6},{5,7},{6,4},{7,5},{8,10},{9,11},{10,... | collective-permute-start | bytes 614408 | tf_op jit(solution)/shard_map/ppermute | solution.py:335
  3.9 13.8 %collective-permute-start.6 = (bf16[40,2560]{1,0:T(8,128)(2,1)S(1)}, bf16[40,2560]{1,0:T(8,128)(2,1)S(1)}, u32[]{:S(2)}, u32[]{:S(2)}) collective-permute-start(bf16[40,2560]{1,0:T(8,128)(2,1)S(1)} %get-tuple-element.32), channel_id=1, source_target_pairs={{0,3},{1,2},{2,1},{3,0},{4,7},{5,6},{6,5},{7,4},{8,11},{9,10},{10,... | collective-permute-start | bytes 614408 | tf_op jit(solution)/shard_map/ppermute | solution.py:335
  5.3 13.7 %collective-permute-start.7 = (bf16[40,2560]{1,0:T(8,128)(2,1)S(1)}, bf16[40,2560]{1,0:T(8,128)(2,1)S(1)}, u32[]{:S(2)}, u32[]{:S(2)}) collective-permute-start(bf16[40,2560]{1,0:T(8,128)(2,1)S(1)} %get-tuple-element.33), channel_id=1, source_target_pairs={{0,4},{1,5},{2,6},{3,7},{4,0},{5,1},{6,2},{7,3},{8,12},{9,13},{10,... | collective-permute-start | bytes 614408 | tf_op jit(solution)/shard_map/ppermute | solution.py:335
  5.6 27.4 %collective-permute-start.8 = (bf16[40,2560]{1,0:T(8,128)(2,1)S(1)}, bf16[40,2560]{1,0:T(8,128)(2,1)S(1)}, u32[]{:S(2)}, u32[]{:S(2)}) collective-permute-start(bf16[40,2560]{1,0:T(8,128)(2,1)S(1)} %get-tuple-element.34), channel_id=1, source_target_pairs={{0,5},{1,4},{2,7},{3,6},{4,1},{5,0},{6,3},{7,2},{8,13},{9,12},{10,... | collective-permute-start | bytes 614408 | tf_op jit(solution)/shard_map/ppermute | solution.py:335
  8.8 40.5 %collective-permute-start = (bf16[40,2560]{1,0:T(8,128)(2,1)S(1)}, bf16[40,2560]{1,0:T(8,128)(2,1)S(1)}, u32[]{:S(2)}, u32[]{:S(2)}) collective-permute-start(bf16[40,2560]{1,0:T(8,128)(2,1)S(1)} %get-tuple-element.24), channel_id=1, source_target_pairs={{0,6},{1,7},{2,4},{3,5},{4,2},{5,3},{6,0},{7,1},{8,14},{9,15},{10,... | collective-permute-start | bytes 614408 | tf_op jit(solution)/shard_map/ppermute | solution.py:335
  14.6 35.0 %collective-permute-start.1 = (bf16[40,2560]{1,0:T(8,128)(2,1)S(1)}, bf16[40,2560]{1,0:T(8,128)(2,1)S(1)}, u32[]{:S(2)}, u32[]{:S(2)}) collective-permute-start(bf16[40,2560]{1,0:T(8,128)(2,1)S(1)} %get-tuple-element.25), channel_id=1, source_target_pairs={{0,7},{1,6},{2,5},{3,4},{4,3},{5,2},{6,1},{7,0},{8,15},{9,14},{10,... | collective-permute-start | bytes 614408 | tf_op jit(solution)/shard_map/ppermute | solution.py:335
  43.2 19.3 %collective-permute-start.9 = (bf16[40,2560]{1,0:T(8,128)(2,1)S(1)}, bf16[40,2560]{1,0:T(8,128)(2,1)S(1)}, u32[]{:S(2)}, u32[]{:S(2)}) collective-permute-start(bf16[40,2560]{1,0:T(8,128)(2,1)S(1)} %get-tuple-element.36), channel_id=1, source_target_pairs={{0,1},{1,0},{2,3},{3,2},{4,5},{5,4},{6,7},{7,6},{8,9},{9,8},{10,11... | collective-permute-start | bytes 614408 | tf_op jit(solution)/shard_map/ppermute | solution.py:335
  43.3 20.0 %collective-permute-start.10 = (bf16[40,2560]{1,0:T(8,128)(2,1)S(1)}, bf16[40,2560]{1,0:T(8,128)(2,1)S(1)}, u32[]{:S(2)}, u32[]{:S(2)}) collective-permute-start(bf16[40,2560]{1,0:T(8,128)(2,1)S(1)} %get-tuple-element.37), channel_id=1, source_target_pairs={{0,2},{1,3},{2,0},{3,1},{4,6},{5,7},{6,4},{7,5},{8,10},{9,11},{10,... | collective-permute-start | bytes 614408 | tf_op jit(solution)/shard_map/ppermute | solution.py:335
  49.3 15.8 %collective-permute-start.11 = (bf16[40,2560]{1,0:T(8,128)(2,1)S(1)}, bf16[40,2560]{1,0:T(8,128)(2,1)S(1)}, u32[]{:S(2)}, u32[]{:S(2)}) collective-permute-start(bf16[40,2560]{1,0:T(8,128)(2,1)S(1)} %get-tuple-element.38), channel_id=1, source_target_pairs={{0,3},{1,2},{2,1},{3,0},{4,7},{5,6},{6,5},{7,4},{8,11},{9,10},{10,... | collective-permute-start | bytes 614408 | tf_op jit(solution)/shard_map/ppermute | solution.py:335
  49.3 15.8 %collective-permute-start.12 = (bf16[40,2560]{1,0:T(8,128)(2,1)S(1)}, bf16[40,2560]{1,0:T(8,128)(2,1)S(1)}, u32[]{:S(2)}, u32[]{:S(2)}) collective-permute-start(bf16[40,2560]{1,0:T(8,128)(2,1)S(1)} %get-tuple-element.39), channel_id=1, source_target_pairs={{0,4},{1,5},{2,6},{3,7},{4,0},{5,1},{6,2},{7,3},{8,12},{9,13},{10,... | collective-permute-start | bytes 614408 | tf_op jit(solution)/shard_map/ppermute | solution.py:335
  49.6 15.0 %copy-start = (s32[128,2]{0,1:T(2,128)S(1)}, s32[128,2]{0,1:T(2,128)}, u32[]{:S(2)}) copy-start(s32[128,2]{0,1:T(2,128)} %param.7) | copy-start | bytes 3076
  49.6 15.0 %copy-start.1 = (f32[128,2]{0,1:T(2,128)S(1)}, f32[128,2]{0,1:T(2,128)}, u32[]{:S(2)}) copy-start(f32[128,2]{0,1:T(2,128)} %param.8) | copy-start | bytes 3076
  49.6 24.6 %collective-permute-start.13 = (bf16[40,2560]{1,0:T(8,128)(2,1)S(1)}, bf16[40,2560]{1,0:T(8,128)(2,1)S(1)}, u32[]{:S(2)}, u32[]{:S(2)}) collective-permute-start(bf16[40,2560]{1,0:T(8,128)(2,1)S(1)} %get-tuple-element.40), channel_id=1, source_target_pairs={{0,5},{1,4},{2,7},{3,6},{4,1},{5,0},{6,3},{7,2},{8,13},{9,12},{10,... | collective-permute-start | bytes 614408 | tf_op jit(solution)/shard_map/ppermute | solution.py:335
  62.5 19.1 %collective-permute-start.2 = (bf16[40,2560]{1,0:T(8,128)(2,1)S(1)}, bf16[40,2560]{1,0:T(8,128)(2,1)S(1)}, u32[]{:S(2)}, u32[]{:S(2)}) collective-permute-start(bf16[40,2560]{1,0:T(8,128)(2,1)S(1)} %get-tuple-element.26), channel_id=1, source_target_pairs={{0,6},{1,7},{2,4},{3,5},{4,2},{5,3},{6,0},{7,1},{8,14},{9,15},{10,... | collective-permute-start | bytes 614408 | tf_op jit(solution)/shard_map/ppermute | solution.py:335
  63.2 21.6 %collective-permute-start.3 = (bf16[40,2560]{1,0:T(8,128)(2,1)S(1)}, bf16[40,2560]{1,0:T(8,128)(2,1)S(1)}, u32[]{:S(2)}, u32[]{:S(2)}) collective-permute-start(bf16[40,2560]{1,0:T(8,128)(2,1)S(1)} %get-tuple-element.27), channel_id=1, source_target_pairs={{0,7},{1,6},{2,5},{3,4},{4,3},{5,2},{6,1},{7,0},{8,15},{9,14},{10,... | collective-permute-start | bytes 614408 | tf_op jit(solution)/shard_map/ppermute | solution.py:335

commit v3 on v2

--- a/solution.py
+++ b/solution.py
@@ -117,21 +117,54 @@
     return spread, slot.astype(jnp.float32)
 
 
-def gather_kernel(members, local_count, me_ref, ids_hbm, tok_hbm, *refs):
-    out_refs = refs[:members]
-    ids_ref, tok_ref, sems = refs[members:]
+def gather_kernel(members, local_count, wanted, me_ref, ids_hbm, tok_hbm, *refs):
+    out_refs = refs[: len(wanted)]
+    ids_ref, tok_ref, sems = refs[len(wanted) :]
     ids_copy = pltpu.make_async_copy(ids_hbm, ids_ref, sems.at[0])
     tok_copy = pltpu.make_async_copy(tok_hbm, tok_ref, sems.at[1])
     ids_copy.start()
     tok_copy.start()
     spread, slot = slot_rows_of(me_ref[0], members, local_count)
+    per_member = local_count * CAP
+
+    def rows_for(value):
+        return jnp.concatenate(
+            [value[m * per_member : (m + 1) * per_member] for m in wanted], axis=0
+        )
+
+    spread, slot = rows_for(spread), rows_for(slot)
     ids_copy.wait()
     chooser = (dot(spread, slot_of_expert(ids_ref)) == slot).astype(jnp.bfloat16)
     tok_copy.wait()
     rows = dot(chooser, tok_ref[...]).astype(jnp.bfloat16)
-    per_member = local_count * CAP
-    for member, out_ref in enumerate(out_refs):
-        out_ref[...] = rows[member * per_member : (member + 1) * per_member]
+    for i, out_ref in enumerate(out_refs):
+        out_ref[...] = rows[i * per_member : (i + 1) * per_member]
+
+
+def ahead_kernel(local_count, mask, me_ref, ids_hbm, tok_hbm, out_ref, ids_ref, tok_ref, sems):
+    ids_copy = pltpu.make_async_copy(ids_hbm, ids_ref, sems.at[0])
+    tok_copy = pltpu.make_async_copy(tok_hbm, tok_ref, sems.at[1])
+    ids_copy.start()
+    tok_copy.start()
+    picks, tok_rows = ids_ref.shape
+    lowest = jnp.bitwise_xor(me_ref[0], mask) * local_count
+    which = iota((-(-local_count // 8) * 8, tok_rows), 0)
+    expert = jnp.where(which < local_count, which + lowest, EXPERTS)
+    earlier = (iota((tok_rows, tok_rows), 0) < iota((tok_rows, tok_rows), 1)).astype(jnp.bfloat16)
+    row = iota((local_count * CAP, tok_rows), 0)
+    ids_copy.wait()
+    hot = ids_ref[0:1, :] == expert
+    for pick in range(1, picks):
+        hot = jnp.logical_or(hot, ids_ref[pick : pick + 1, :] == expert)
+    slot = jnp.where(hot, dot(hot.astype(jnp.bfloat16), earlier), -1.0).astype(jnp.int32)
+    taken = jnp.full(row.shape, -1, jnp.int32)
+    for i in range(local_count):
+        mine = jnp.where(slot[i : i + 1] < 0, -1, slot[i : i + 1] + i * CAP)
+        inside = jnp.logical_and(row >= i * CAP, row < (i + 1) * CAP)
+        taken = jnp.where(inside, mine, taken)
+    chooser = (taken == row).astype(jnp.bfloat16)
+    tok_copy.wait()
+    out_ref[...] = dot(chooser, tok_ref[...]).astype(jnp.bfloat16)
 
 
 def mixer_kernel(members, local_count, groups, me_ref, ids_ref, wts_ref, *out_refs):
@@ -228,6 +261,22 @@
     refs[-1][...] = mixed.astype(refs[-1].dtype)
 
 
+def last_kernel(count, *refs):
+    share_ref, row_refs, total_ref = refs[0], refs[1 : 1 + count], refs[1 + count]
+    out_hbm, held, sems = refs[2 + count :]
+    pieces, _, width = held.shape
+    copies = []
+    for piece in range(pieces):
+        span = slice(piece * width, (piece + 1) * width)
+        rows = jnp.concatenate([ref[:, span] for ref in row_refs] * 2, axis=0)
+        held[piece] = (dot(share_ref[...], rows) + total_ref[:, span]).astype(held.dtype)
+        copy = pltpu.make_async_copy(held.at[piece], out_hbm.at[:, span], sems.at[piece])
+        copy.start()
+        copies.append(copy)
+    for copy in copies:
+        copy.wait()
+
+
 def whole(*_):
     return pl.BlockSpec(memory_space=VMEM)
 
@@ -240,21 +289,35 @@
     return pltpu.CompilerParams(vmem_limit_bytes=8 * 1024 * 1024, **kwargs)
 
 
-def gather(me, ids, tokens, members, local_count):
+def gather(me, ids, tokens, members, local_count, wanted):
     per_member = local_count * CAP
     model_width = tokens.shape[1]
     return pl.pallas_call(
-        functools.partial(gather_kernel, members, local_count),
-        out_shape=[jax.ShapeDtypeStruct((per_member, model_width), jnp.bfloat16)] * members,
+        functools.partial(gather_kernel, members, local_count, wanted),
+        out_shape=[jax.ShapeDtypeStruct((per_member, model_width), jnp.bfloat16)] * len(wanted),
         in_specs=[pl.BlockSpec(memory_space=pltpu.SMEM)] + [pl.BlockSpec(memory_space=pltpu.HBM)] * 2,
-        out_specs=[whole()] * members,
+        out_specs=[whole()] * len(wanted),
         scratch_shapes=[
             VMEM(ids.shape, ids.dtype),
             VMEM(tokens.shape, tokens.dtype),
             pltpu.SemaphoreType.DMA((2,)),
         ],
         compiler_params=small(),
-        name="gather",
+    )(me, in_hbm(ids), in_hbm(tokens))
+
+
+def gather_ahead(me, ids, tokens, mask, local_count):
+    return pl.pallas_call(
+        functools.partial(ahead_kernel, local_count, mask),
+        out_shape=jax.ShapeDtypeStruct((local_count * CAP, tokens.shape[1]), jnp.bfloat16),
+        in_specs=[pl.BlockSpec(memory_space=pltpu.SMEM)] + [pl.BlockSpec(memory_space=pltpu.HBM)] * 2,
+        out_specs=whole(),
+        scratch_shapes=[
+            VMEM(ids.shape, ids.dtype),
+            VMEM(tokens.shape, tokens.dtype),
+            pltpu.SemaphoreType.DMA((2,)),
+        ],
+        compiler_params=small(),
     )(me, in_hbm(ids), in_hbm(tokens))
 
 
@@ -272,6 +335,22 @@
         compiler_params=small(),
         name="mixer",
     )(me, ids, wts)
+
+
+def mix_out(shares, rows, total, dtype, pieces):
+    tok_rows, model_width = total.shape
+    pieces = pieces if model_width % (128 * pieces) == 0 else 1
+    return pl.pallas_call(
+        functools.partial(last_kernel, len(rows)),
+        out_shape=jax.ShapeDtypeStruct(total.shape, dtype),
+        in_specs=[whole()] * (len(rows) + 2),
+        out_specs=pl.BlockSpec(memory_space=pltpu.HBM),
+        scratch_shapes=[
+            VMEM((pieces, tok_rows, model_width // pieces), dtype),
+            pltpu.SemaphoreType.DMA((pieces,)),
+        ],
+        compiler_params=small(),
+    )(shares, *rows, total)
 
 
 def block_of(size, wanted):
@@ -334,7 +413,11 @@
     def move(value, mask):
         return lax.ppermute(value, "expert", [(i, i ^ mask) for i in range(members)])
 
-    sent = gather(me, ids, tokens, members, local_count)
+    ahead = members // 2
+    rest = tuple(m for m in range(members) if m != ahead)
+    sent = {ahead: gather_ahead(me, ids, tokens, ahead, local_count)}
+    rows = gather(me, ids, tokens, members, local_count, rest)
+    sent.update(zip(rest, rows))
     arrived = {m: move(sent[m], m) if m else sent[0] for m in range(members)}
     shares = mixer(me, ids, wts, members, local_count, (early, last))
     back = {}
@@ -343,7 +426,7 @@
         for m, value in zip(group, done):
             back[m] = move(value, m) if m else value
     total = mix(shares[0], [back[m] for m in early], None, jnp.float32)
-    return mix(shares[1], [back[m] for m in last], total, jnp.bfloat16)
+    return mix_out(shares[1], [back[m] for m in last], total, jnp.bfloat16, 4)
 
 
 def per_device(tokens, expert_ids, gate_weights, w_gate, w_up, w_down):

time: 86.1 us -> 86.2 us (level)
  the two profiles are of different devices: /device:TPU:22 before, /device:TPU:10 now
where the time goes in v3:
time: 86.2 us; the launch traced here: 86.1 us
  waiting for transfers between devices  40.9 us (47%)
  Pallas kernels  24.6 us (29%)
  starting transfers between devices  20.5 us (24%)
    ppermute x14, waiting for transfers between devices, move(): lax.ppermute(value, 'expert', [(i, i ^ mask) for i in range(members)])  40.9 us
    ppermute x14, starting transfers between devices, move(): lax.ppermute(value, 'expert', [(i, i ^ mask) for i in range(members)])  20.5 us
    pallas_call x2, Pallas kernels, mlp(): pl.pallas_call(functools.partial(mlp_kernel, count, local_count, depth_bl...  19.5 us
  transfers between devices with their start and end apart: 14, of which 6 were waited for; matrix products, arithmetic and copies ran while one was open for 0% of the time, Pallas kernels for 26%

profile of v3, /device:TPU:10, one launch (start us, length us, event | category | flops | bytes accessed | tf_op | source)
XLA Modules:
  0.0 86.1 jit_solution(6583800837914691942)
XLA Ops:
  0.0 1.4 %shard_map.66 = bf16[40,2560]{1,0:T(8,128)(2,1)S(1)} custom-call(s32[1]{0:T(128)} %bitcast.me_ref, s32[2,128]{1,0:T(2,128)} %bitcast.3, bf16[128,2560]{1,0:T(8,128)(2,1)} %tok_hbm.3), custom_call_target="tpu_custom_call" | custom-call | tf_op jit(solution)/shard_map/pallas_call | solution.py:310
  1.4 2.7 %collective-permute-start.7 = (bf16[40,2560]{1,0:T(8,128)(2,1)S(1)}, bf16[40,2560]{1,0:T(8,128)(2,1)S(1)}, u32[]{:S(2)}, u32[]{:S(2)}) collective-permute-start(bf16[40,2560]{1,0:T(8,128)(2,1)S(1)} %shard_map.66), channel_id=1, source_target_pairs={{0,4},{1,5},{2,6},{3,7},{4,0},{5,1},{6,2},{7,3},{8,12},{9,13},{10,... | collective-permute-start | bytes 614408 | tf_op jit(solution)/shard_map/ppermute | solution.py:414
  4.0 1.6 %shard_map.64 = (bf16[40,2560]{1,0:T(8,128)(2,1)S(1)}, bf16[40,2560]{1,0:T(8,128)(2,1)S(1)}, bf16[40,2560]{1,0:T(8,128)(2,1)S(1)}, bf16[40,2560]{1,0:T(8,128)(2,...) custom-call(s32[1]{0:T(128)} %bitcast.me_ref, s32[2,128]{1,0:T(2,128)} %bitcast.4, ...), custom_call_target="tpu_custom_call" | custom-call | tf_op jit(solution)/shard_map/pallas_call | solution.py:295
  5.7 1.6 %collective-permute-start.4 = (bf16[40,2560]{1,0:T(8,128)(2,1)S(1)}, bf16[40,2560]{1,0:T(8,128)(2,1)S(1)}, u32[]{:S(2)}, u32[]{:S(2)}) collective-permute-start(bf16[40,2560]{1,0:T(8,128)(2,1)S(1)} %get-tuple-element.29), channel_id=1, source_target_pairs={{0,1},{1,0},{2,3},{3,2},{4,5},{5,4},{6,7},{7,6},{8,9},{9,8},{10,11... | collective-permute-start | bytes 614408 | tf_op jit(solution)/shard_map/ppermute | solution.py:414
  7.3 0.5 collective-permute-start.5
  7.7 1.5 %collective-permute-start.6 = (bf16[40,2560]{1,0:T(8,128)(2,1)S(1)}, bf16[40,2560]{1,0:T(8,128)(2,1)S(1)}, u32[]{:S(2)}, u32[]{:S(2)}) collective-permute-start(bf16[40,2560]{1,0:T(8,128)(2,1)S(1)} %get-tuple-element.31), channel_id=1, source_target_pairs={{0,3},{1,2},{2,1},{3,0},{4,7},{5,6},{6,5},{7,4},{8,11},{9,10},{10,... | collective-permute-start | bytes 614408 | tf_op jit(solution)/shard_map/ppermute | solution.py:414
  9.2 1.3 %collective-permute-start.8 = (bf16[40,2560]{1,0:T(8,128)(2,1)S(1)}, bf16[40,2560]{1,0:T(8,128)(2,1)S(1)}, u32[]{:S(2)}, u32[]{:S(2)}) collective-permute-start(bf16[40,2560]{1,0:T(8,128)(2,1)S(1)} %get-tuple-element.32), channel_id=1, source_target_pairs={{0,5},{1,4},{2,7},{3,6},{4,1},{5,0},{6,3},{7,2},{8,13},{9,12},{10,... | collective-permute-start | bytes 614408 | tf_op jit(solution)/shard_map/ppermute | solution.py:414
  10.5 2.2 %collective-permute-done.7.refs_4_ = bf16[40,2560]{1,0:T(8,128)(2,1)S(1)} collective-permute-done((bf16[40,2560]{1,0:T(8,128)(2,1)S(1)}, bf16[40,2560]{1,0:T(8,128)(2,1)S(1)}, u32[]{:S(2)}, u32[]{:S(2)}) %collective-permute-start.7) | collective-permute-done | bytes 204832 | tf_op jit(solution)/shard_map/ppermute | solution.py:414
  12.8 0.4 collective-permute-start
  13.2 0.0 collective-permute-done.4.refs_1_
  13.2 2.5 %collective-permute-start.1 = (bf16[40,2560]{1,0:T(8,128)(2,1)S(1)}, bf16[40,2560]{1,0:T(8,128)(2,1)S(1)}, u32[]{:S(2)}, u32[]{:S(2)}) collective-permute-start(bf16[40,2560]{1,0:T(8,128)(2,1)S(1)} %get-tuple-element.24), channel_id=1, source_target_pairs={{0,7},{1,6},{2,5},{3,4},{4,3},{5,2},{6,1},{7,0},{8,15},{9,14},{10,... | collective-permute-start | bytes 614408 | tf_op jit(solution)/shard_map/ppermute | solution.py:414
  15.8 4.3 %collective-permute-done.5.refs_2_ = bf16[40,2560]{1,0:T(8,128)(2,1)S(1)} collective-permute-done((bf16[40,2560]{1,0:T(8,128)(2,1)S(1)}, bf16[40,2560]{1,0:T(8,128)(2,1)S(1)}, u32[]{:S(2)}, u32[]{:S(2)}) %collective-permute-start.5) | collective-permute-done | bytes 204832 | tf_op jit(solution)/shard_map/ppermute | solution.py:414
  20.0 12.3 %collective-permute-done.6.refs_3_ = bf16[40,2560]{1,0:T(8,128)(2,1)S(1)} collective-permute-done((bf16[40,2560]{1,0:T(8,128)(2,1)S(1)}, bf16[40,2560]{1,0:T(8,128)(2,1)S(1)}, u32[]{:S(2)}, u32[]{:S(2)}) %collective-permute-start.6) | collective-permute-done | bytes 204832 | tf_op jit(solution)/shard_map/ppermute | solution.py:414
  32.3 0.0 collective-permute-done.8.refs_5_
  32.3 10.2 %shard_map.67 = (bf16[40,2560]{1,0:T(8,128)(2,1)S(1)}, bf16[40,2560]{1,0:T(8,128)(2,1)S(1)}, bf16[40,2560]{1,0:T(8,128)(2,1)S(1)}, bf16[40,2560]{1,0:T(8,128)(2,...) custom-call(bf16[40,2560]{1,0:T(8,128)(2,1)S(1)} %get-tuple-element.28.refs_0_, ...), custom_call_target="tpu_custom_call" | custom-call | flops 5662310400 | bytes 23592960 | tf_op jit(solution)/shard_map/pallas_call | solution.py:366
  42.5 0.6 collective-permute-start.9
  43.1 3.4 %collective-permute-start.10 = (bf16[40,2560]{1,0:T(8,128)(2,1)S(1)}, bf16[40,2560]{1,0:T(8,128)(2,1)S(1)}, u32[]{:S(2)}, u32[]{:S(2)}) collective-permute-start(bf16[40,2560]{1,0:T(8,128)(2,1)S(1)} %get-tuple-element.35), channel_id=1, source_target_pairs={{0,2},{1,3},{2,0},{3,1},{4,6},{5,7},{6,4},{7,5},{8,10},{9,11},{10,... | collective-permute-start | bytes 614408 | tf_op jit(solution)/shard_map/ppermute | solution.py:414
  46.5 0.0 collective-permute-start.11
  46.5 0.0 collective-permute-done.refs_0_
  46.5 2.9 %collective-permute-start.12 = (bf16[40,2560]{1,0:T(8,128)(2,1)S(1)}, bf16[40,2560]{1,0:T(8,128)(2,1)S(1)}, u32[]{:S(2)}, u32[]{:S(2)}) collective-permute-start(bf16[40,2560]{1,0:T(8,128)(2,1)S(1)} %get-tuple-element.37), channel_id=1, source_target_pairs={{0,4},{1,5},{2,6},{3,7},{4,0},{5,1},{6,2},{7,3},{8,12},{9,13},{10,... | collective-permute-start | bytes 614408 | tf_op jit(solution)/shard_map/ppermute | solution.py:414
  49.4 0.0 collective-permute-done.1.refs_1_
  49.4 0.0 copy-start
  49.4 0.0 copy-start.1
  49.4 1.0 %collective-permute-start.13 = (bf16[40,2560]{1,0:T(8,128)(2,1)S(1)}, bf16[40,2560]{1,0:T(8,128)(2,1)S(1)}, u32[]{:S(2)}, u32[]{:S(2)}) collective-permute-start(bf16[40,2560]{1,0:T(8,128)(2,1)S(1)} %get-tuple-element.38), channel_id=1, source_target_pairs={{0,5},{1,4},{2,7},{3,6},{4,1},{5,0},{6,3},{7,2},{8,13},{9,12},{10,... | collective-permute-start | bytes 614408 | tf_op jit(solution)/shard_map/ppermute | solution.py:414
  50.4 9.3 %shard_map.65 = (bf16[40,2560]{1,0:T(8,128)(2,1)S(1)}, bf16[40,2560]{1,0:T(8,128)(2,1)S(1)}) custom-call(bf16[40,2560]{1,0:T(8,128)(2,1)S(1)} %collective-permute-done.refs_0_, bf16[40,2560]{1,0:T(8,128)(2,1)S(1)} %collective-permute-done.1.refs_1_, bf16[2560,1536]{1,0:T(8,128)(2,1)} %refs_6_.1, bf16[2560,1536]{1,0:T(8,128)(2,1)} %refs_7_.1, ...), custom_call_target="tpu_custom_call" | custom-call | flops 1887436800 | bytes 23592960 | tf_op jit(solution)/shard_map/pallas_call | solution.py:366
  59.8 0.0 collective-permute-done.9.refs_2_
  59.8 1.4 %collective-permute-start.2 = (bf16[40,2560]{1,0:T(8,128)(2,1)S(1)}, bf16[40,2560]{1,0:T(8,128)(2,1)S(1)}, u32[]{:S(2)}, u32[]{:S(2)}) collective-permute-start(bf16[40,2560]{1,0:T(8,128)(2,1)S(1)} %get-tuple-element.25), channel_id=1, source_target_pairs={{0,6},{1,7},{2,4},{3,5},{4,2},{5,3},{6,0},{7,1},{8,14},{9,15},{10,... | collective-permute-start | bytes 614408 | tf_op jit(solution)/shard_map/ppermute | solution.py:414
  61.2 0.0 collective-permute-done.10.refs_3_
  61.2 0.6 collective-permute-start.3
  61.8 0.0 copy-done
  61.8 0.0 copy-done.1
  61.8 0.5 mixer.1
  62.4 0.0 collective-permute-done.11.refs_4_
  62.4 0.0 collective-permute-done.12.refs_5_
  62.4 12.5 %collective-permute-done.13.refs_6_ = bf16[40,2560]{1,0:T(8,128)(2,1)S(1)} collective-permute-done((bf16[40,2560]{1,0:T(8,128)(2,1)S(1)}, bf16[40,2560]{1,0:T(8,128)(2,1)S(1)}, u32[]{:S(2)}, u32[]{:S(2)}) %collective-permute-start.13) | collective-permute-done | bytes 204832 | tf_op jit(solution)/shard_map/ppermute | solution.py:414
  74.9 0.5 shard_map.68.refs_3_
  75.4 6.3 %collective-permute-done.2.refs_1_ = bf16[40,2560]{1,0:T(8,128)(2,1)S(1)} collective-permute-done((bf16[40,2560]{1,0:T(8,128)(2,1)S(1)}, bf16[40,2560]{1,0:T(8,128)(2,1)S(1)}, u32[]{:S(2)}, u32[]{:S(2)}) %collective-permute-start.2) | collective-permute-done | bytes 204832 | tf_op jit(solution)/shard_map/ppermute | solution.py:414
  81.7 3.3 %collective-permute-done.3.refs_2_ = bf16[40,2560]{1,0:T(8,128)(2,1)S(1)} collective-permute-done((bf16[40,2560]{1,0:T(8,128)(2,1)S(1)}, bf16[40,2560]{1,0:T(8,128)(2,1)S(1)}, u32[]{:S(2)}, u32[]{:S(2)}) %collective-permute-start.3) | collective-permute-done | bytes 204832 | tf_op jit(solution)/shard_map/ppermute | solution.py:414
  85.0 1.1 %shard_map.69 = bf16[128,2560]{1,0:T(8,128)(2,1)} custom-call(bf16[128,160]{1,0:T(8,128)(2,1)S(1)} %get-tuple-element.22.refs_0_, bf16[40,2560]{1,0:T(8,128)(2,1)S(1)} %collective-permute-done.2.refs_1_, bf16[40,2560]{1,0:T(8,128)(2,1)S(1)} %collective-permute-done.3.refs_2_, f32[128,2560]{1,0:T(8,128)S(1)} %shard_map.68.refs_3_), custom_call_target="tpu_custom_call" | custom-call | tf_op jit(solution)/shard_map/pallas_call | solution.py:343
Async XLA Ops:
  1.4 11.4 %collective-permute-start.7 = (bf16[40,2560]{1,0:T(8,128)(2,1)S(1)}, bf16[40,2560]{1,0:T(8,128)(2,1)S(1)}, u32[]{:S(2)}, u32[]{:S(2)}) collective-permute-start(bf16[40,2560]{1,0:T(8,128)(2,1)S(1)} %shard_map.66), channel_id=1, source_target_pairs={{0,4},{1,5},{2,6},{3,7},{4,0},{5,1},{6,2},{7,3},{8,12},{9,13},{10,... | collective-permute-start | bytes 614408 | tf_op jit(solution)/shard_map/ppermute | solution.py:414
  5.7 7.6 %collective-permute-start.4 = (bf16[40,2560]{1,0:T(8,128)(2,1)S(1)}, bf16[40,2560]{1,0:T(8,128)(2,1)S(1)}, u32[]{:S(2)}, u32[]{:S(2)}) collective-permute-start(bf16[40,2560]{1,0:T(8,128)(2,1)S(1)} %get-tuple-element.29), channel_id=1, source_target_pairs={{0,1},{1,0},{2,3},{3,2},{4,5},{5,4},{6,7},{7,6},{8,9},{9,8},{10,11... | collective-permute-start | bytes 614408 | tf_op jit(solution)/shard_map/ppermute | solution.py:414
  7.3 12.8 %collective-permute-start.5 = (bf16[40,2560]{1,0:T(8,128)(2,1)S(1)}, bf16[40,2560]{1,0:T(8,128)(2,1)S(1)}, u32[]{:S(2)}, u32[]{:S(2)}) collective-permute-start(bf16[40,2560]{1,0:T(8,128)(2,1)S(1)} %get-tuple-element.30), channel_id=1, source_target_pairs={{0,2},{1,3},{2,0},{3,1},{4,6},{5,7},{6,4},{7,5},{8,10},{9,11},{10,... | collective-permute-start | bytes 614408 | tf_op jit(solution)/shard_map/ppermute | solution.py:414
  7.7 24.6 %collective-permute-start.6 = (bf16[40,2560]{1,0:T(8,128)(2,1)S(1)}, bf16[40,2560]{1,0:T(8,128)(2,1)S(1)}, u32[]{:S(2)}, u32[]{:S(2)}) collective-permute-start(bf16[40,2560]{1,0:T(8,128)(2,1)S(1)} %get-tuple-element.31), channel_id=1, source_target_pairs={{0,3},{1,2},{2,1},{3,0},{4,7},{5,6},{6,5},{7,4},{8,11},{9,10},{10,... | collective-permute-start | bytes 614408 | tf_op jit(solution)/shard_map/ppermute | solution.py:414
  9.2 23.1 %collective-permute-start.8 = (bf16[40,2560]{1,0:T(8,128)(2,1)S(1)}, bf16[40,2560]{1,0:T(8,128)(2,1)S(1)}, u32[]{:S(2)}, u32[]{:S(2)}) collective-permute-start(bf16[40,2560]{1,0:T(8,128)(2,1)S(1)} %get-tuple-element.32), channel_id=1, source_target_pairs={{0,5},{1,4},{2,7},{3,6},{4,1},{5,0},{6,3},{7,2},{8,13},{9,12},{10,... | collective-permute-start | bytes 614408 | tf_op jit(solution)/shard_map/ppermute | solution.py:414
  12.8 33.7 %collective-permute-start = (bf16[40,2560]{1,0:T(8,128)(2,1)S(1)}, bf16[40,2560]{1,0:T(8,128)(2,1)S(1)}, u32[]{:S(2)}, u32[]{:S(2)}) collective-permute-start(bf16[40,2560]{1,0:T(8,128)(2,1)S(1)} %get-tuple-element.23), channel_id=1, source_target_pairs={{0,6},{1,7},{2,4},{3,5},{4,2},{5,3},{6,0},{7,1},{8,14},{9,15},{10,... | collective-permute-start | bytes 614408 | tf_op jit(solution)/shard_map/ppermute | solution.py:414
  13.2 36.2 %collective-permute-start.1 = (bf16[40,2560]{1,0:T(8,128)(2,1)S(1)}, bf16[40,2560]{1,0:T(8,128)(2,1)S(1)}, u32[]{:S(2)}, u32[]{:S(2)}) collective-permute-start(bf16[40,2560]{1,0:T(8,128)(2,1)S(1)} %get-tuple-element.24), channel_id=1, source_target_pairs={{0,7},{1,6},{2,5},{3,4},{4,3},{5,2},{6,1},{7,0},{8,15},{9,14},{10,... | collective-permute-start | bytes 614408 | tf_op jit(solution)/shard_map/ppermute | solution.py:414
  42.5 17.3 %collective-permute-start.9 = (bf16[40,2560]{1,0:T(8,128)(2,1)S(1)}, bf16[40,2560]{1,0:T(8,128)(2,1)S(1)}, u32[]{:S(2)}, u32[]{:S(2)}) collective-permute-start(bf16[40,2560]{1,0:T(8,128)(2,1)S(1)} %get-tuple-element.34), channel_id=1, source_target_pairs={{0,1},{1,0},{2,3},{3,2},{4,5},{5,4},{6,7},{7,6},{8,9},{9,8},{10,11... | collective-permute-start | bytes 614408 | tf_op jit(solution)/shard_map/ppermute | solution.py:414
  43.1 18.1 %collective-permute-start.10 = (bf16[40,2560]{1,0:T(8,128)(2,1)S(1)}, bf16[40,2560]{1,0:T(8,128)(2,1)S(1)}, u32[]{:S(2)}, u32[]{:S(2)}) collective-permute-start(bf16[40,2560]{1,0:T(8,128)(2,1)S(1)} %get-tuple-element.35), channel_id=1, source_target_pairs={{0,2},{1,3},{2,0},{3,1},{4,6},{5,7},{6,4},{7,5},{8,10},{9,11},{10,... | collective-permute-start | bytes 614408 | tf_op jit(solution)/shard_map/ppermute | solution.py:414
  46.5 15.9 %collective-permute-start.11 = (bf16[40,2560]{1,0:T(8,128)(2,1)S(1)}, bf16[40,2560]{1,0:T(8,128)(2,1)S(1)}, u32[]{:S(2)}, u32[]{:S(2)}) collective-permute-start(bf16[40,2560]{1,0:T(8,128)(2,1)S(1)} %get-tuple-element.36), channel_id=1, source_target_pairs={{0,3},{1,2},{2,1},{3,0},{4,7},{5,6},{6,5},{7,4},{8,11},{9,10},{10,... | collective-permute-start | bytes 614408 | tf_op jit(solution)/shard_map/ppermute | solution.py:414
  46.5 15.9 %collective-permute-start.12 = (bf16[40,2560]{1,0:T(8,128)(2,1)S(1)}, bf16[40,2560]{1,0:T(8,128)(2,1)S(1)}, u32[]{:S(2)}, u32[]{:S(2)}) collective-permute-start(bf16[40,2560]{1,0:T(8,128)(2,1)S(1)} %get-tuple-element.37), channel_id=1, source_target_pairs={{0,4},{1,5},{2,6},{3,7},{4,0},{5,1},{6,2},{7,3},{8,12},{9,13},{10,... | collective-permute-start | bytes 614408 | tf_op jit(solution)/shard_map/ppermute | solution.py:414
  49.4 12.5 %copy-start = (s32[128,2]{0,1:T(2,128)S(1)}, s32[128,2]{0,1:T(2,128)}, u32[]{:S(2)}) copy-start(s32[128,2]{0,1:T(2,128)} %param.7) | copy-start | bytes 3076
  49.4 12.5 %copy-start.1 = (f32[128,2]{0,1:T(2,128)S(1)}, f32[128,2]{0,1:T(2,128)}, u32[]{:S(2)}) copy-start(f32[128,2]{0,1:T(2,128)} %param.8) | copy-start | bytes 3076
  49.4 25.5 %collective-permute-start.13 = (bf16[40,2560]{1,0:T(8,128)(2,1)S(1)}, bf16[40,2560]{1,0:T(8,128)(2,1)S(1)}, u32[]{:S(2)}, u32[]{:S(2)}) collective-permute-start(bf16[40,2560]{1,0:T(8,128)(2,1)S(1)} %get-tuple-element.38), channel_id=1, source_target_pairs={{0,5},{1,4},{2,7},{3,6},{4,1},{5,0},{6,3},{7,2},{8,13},{9,12},{10,... | collective-permute-start | bytes 614408 | tf_op jit(solution)/shard_map/ppermute | solution.py:414
  59.8 21.9 %collective-permute-start.2 = (bf16[40,2560]{1,0:T(8,128)(2,1)S(1)}, bf16[40,2560]{1,0:T(8,128)(2,1)S(1)}, u32[]{:S(2)}, u32[]{:S(2)}) collective-permute-start(bf16[40,2560]{1,0:T(8,128)(2,1)S(1)} %get-tuple-element.25), channel_id=1, source_target_pairs={{0,6},{1,7},{2,4},{3,5},{4,2},{5,3},{6,0},{7,1},{8,14},{9,15},{10,... | collective-permute-start | bytes 614408 | tf_op jit(solution)/shard_map/ppermute | solution.py:414
  61.2 23.8 %collective-permute-start.3 = (bf16[40,2560]{1,0:T(8,128)(2,1)S(1)}, bf16[40,2560]{1,0:T(8,128)(2,1)S(1)}, u32[]{:S(2)}, u32[]{:S(2)}) collective-permute-start(bf16[40,2560]{1,0:T(8,128)(2,1)S(1)} %get-tuple-element.26), channel_id=1, source_target_pairs={{0,7},{1,6},{2,5},{3,4},{4,3},{5,2},{6,1},{7,0},{8,15},{9,14},{10,... | collective-permute-start | bytes 614408 | tf_op jit(solution)/shard_map/ppermute | solution.py:414

commit v4 on v2

--- a/solution.py
+++ b/solution.py
@@ -117,21 +117,28 @@
     return spread, slot.astype(jnp.float32)
 
 
-def gather_kernel(members, local_count, me_ref, ids_hbm, tok_hbm, *refs):
-    out_refs = refs[:members]
-    ids_ref, tok_ref, sems = refs[members:]
+def gather_kernel(members, local_count, wanted, me_ref, ids_hbm, tok_hbm, *refs):
+    out_refs = refs[: len(wanted)]
+    ids_ref, tok_ref, sems = refs[len(wanted) :]
     ids_copy = pltpu.make_async_copy(ids_hbm, ids_ref, sems.at[0])
     tok_copy = pltpu.make_async_copy(tok_hbm, tok_ref, sems.at[1])
     ids_copy.start()
     tok_copy.start()
     spread, slot = slot_rows_of(me_ref[0], members, local_count)
+    per_member = local_count * CAP
+
+    def rows_for(value):
+        return jnp.concatenate(
+            [value[m * per_member : (m + 1) * per_member] for m in wanted], axis=0
+        )
+
+    spread, slot = rows_for(spread), rows_for(slot)
     ids_copy.wait()
     chooser = (dot(spread, slot_of_expert(ids_ref)) == slot).astype(jnp.bfloat16)
     tok_copy.wait()
     rows = dot(chooser, tok_ref[...]).astype(jnp.bfloat16)
-    per_member = local_count * CAP
-    for member, out_ref in enumerate(out_refs):
-        out_ref[...] = rows[member * per_member : (member + 1) * per_member]
+    for i, out_ref in enumerate(out_refs):
+        out_ref[...] = rows[i * per_member : (i + 1) * per_member]
 
 
 def mixer_kernel(members, local_count, groups, me_ref, ids_ref, wts_ref, *out_refs):
@@ -240,21 +247,20 @@
     return pltpu.CompilerParams(vmem_limit_bytes=8 * 1024 * 1024, **kwargs)
 
 
-def gather(me, ids, tokens, members, local_count):
+def gather(me, ids, tokens, members, local_count, wanted):
     per_member = local_count * CAP
     model_width = tokens.shape[1]
     return pl.pallas_call(
-        functools.partial(gather_kernel, members, local_count),
-        out_shape=[jax.ShapeDtypeStruct((per_member, model_width), jnp.bfloat16)] * members,
+        functools.partial(gather_kernel, members, local_count, wanted),
+        out_shape=[jax.ShapeDtypeStruct((per_member, model_width), jnp.bfloat16)] * len(wanted),
         in_specs=[pl.BlockSpec(memory_space=pltpu.SMEM)] + [pl.BlockSpec(memory_space=pltpu.HBM)] * 2,
-        out_specs=[whole()] * members,
+        out_specs=[whole()] * len(wanted),
         scratch_shapes=[
             VMEM(ids.shape, ids.dtype),
             VMEM(tokens.shape, tokens.dtype),
             pltpu.SemaphoreType.DMA((2,)),
         ],
         compiler_params=small(),
-        name="gather",
     )(me, in_hbm(ids), in_hbm(tokens))
 
 
@@ -334,7 +340,12 @@
     def move(value, mask):
         return lax.ppermute(value, "expert", [(i, i ^ mask) for i in range(members)])
 
-    sent = gather(me, ids, tokens, members, local_count)
+    ahead = (members // 2,)
+    rest = tuple(m for m in range(members) if m not in ahead)
+    sent = {}
+    for wanted in (ahead, rest):
+        rows = gather(me, ids, tokens, members, local_count, wanted)
+        sent.update(zip(wanted, rows))
     arrived = {m: move(sent[m], m) if m else sent[0] for m in range(members)}
     shares = mixer(me, ids, wts, members, local_count, (early, last))
     back = {}

time: 86.1 us -> 86.3 us (level)
  the two profiles are of different devices: /device:TPU:22 before, /device:TPU:10 now
where the time goes in v4:
time: 86.3 us; the launch traced here: 86.2 us
  waiting for transfers between devices  40.9 us (47%)
  Pallas kernels  24.7 us (29%)
  starting transfers between devices  20.5 us (24%)
    ppermute x14, waiting for transfers between devices, move(): lax.ppermute(value, 'expert', [(i, i ^ mask) for i in range(members)])  40.9 us
    ppermute x14, starting transfers between devices, move(): lax.ppermute(value, 'expert', [(i, i ^ mask) for i in range(members)])  20.5 us
    pallas_call x2, Pallas kernels, mlp(): pl.pallas_call(functools.partial(mlp_kernel, count, local_count, depth_bl...  19.5 us
    pallas_call x2, Pallas kernels, gather(): pl.pallas_call(functools.partial(gather_kernel, members, local_count, wan...  3.01 us
  transfers between devices with their start and end apart: 14, of which 6 were waited for; matrix products, arithmetic and copies ran while one was open for 0% of the time, Pallas kernels for 26%

profile of v4, /device:TPU:10, one launch (start us, length us, event | category | flops | bytes accessed | tf_op | source)
XLA Modules:
  0.0 86.2 jit_solution(1654531715963723512)
XLA Ops:
  0.0 1.4 %shard_map.66 = bf16[40,2560]{1,0:T(8,128)(2,1)S(1)} custom-call(s32[1]{0:T(128)} %bitcast.me_ref, s32[2,128]{1,0:T(2,128)} %bitcast.3, bf16[128,2560]{1,0:T(8,128)(2,1)} %tok_hbm.3), custom_call_target="tpu_custom_call" | custom-call | tf_op jit(solution)/shard_map/pallas_call | solution.py:253
  1.4 2.7 %collective-permute-start.7 = (bf16[40,2560]{1,0:T(8,128)(2,1)S(1)}, bf16[40,2560]{1,0:T(8,128)(2,1)S(1)}, u32[]{:S(2)}, u32[]{:S(2)}) collective-permute-start(bf16[40,2560]{1,0:T(8,128)(2,1)S(1)} %shard_map.66), channel_id=1, source_target_pairs={{0,4},{1,5},{2,6},{3,7},{4,0},{5,1},{6,2},{7,3},{8,12},{9,13},{10,... | collective-permute-start | bytes 614408 | tf_op jit(solution)/shard_map/ppermute | solution.py:341
  4.0 1.7 %shard_map.64 = (bf16[40,2560]{1,0:T(8,128)(2,1)S(1)}, bf16[40,2560]{1,0:T(8,128)(2,1)S(1)}, bf16[40,2560]{1,0:T(8,128)(2,1)S(1)}, bf16[40,2560]{1,0:T(8,128)(2,...) custom-call(s32[1]{0:T(128)} %bitcast.me_ref, s32[2,128]{1,0:T(2,128)} %bitcast.4, ...), custom_call_target="tpu_custom_call" | custom-call | tf_op jit(solution)/shard_map/pallas_call | solution.py:253
  5.7 1.6 %collective-permute-start.4 = (bf16[40,2560]{1,0:T(8,128)(2,1)S(1)}, bf16[40,2560]{1,0:T(8,128)(2,1)S(1)}, u32[]{:S(2)}, u32[]{:S(2)}) collective-permute-start(bf16[40,2560]{1,0:T(8,128)(2,1)S(1)} %get-tuple-element.29), channel_id=1, source_target_pairs={{0,1},{1,0},{2,3},{3,2},{4,5},{5,4},{6,7},{7,6},{8,9},{9,8},{10,11... | collective-permute-start | bytes 614408 | tf_op jit(solution)/shard_map/ppermute | solution.py:341
  7.3 0.4 collective-permute-start.5
  7.7 1.5 %collective-permute-start.6 = (bf16[40,2560]{1,0:T(8,128)(2,1)S(1)}, bf16[40,2560]{1,0:T(8,128)(2,1)S(1)}, u32[]{:S(2)}, u32[]{:S(2)}) collective-permute-start(bf16[40,2560]{1,0:T(8,128)(2,1)S(1)} %get-tuple-element.31), channel_id=1, source_target_pairs={{0,3},{1,2},{2,1},{3,0},{4,7},{5,6},{6,5},{7,4},{8,11},{9,10},{10,... | collective-permute-start | bytes 614408 | tf_op jit(solution)/shard_map/ppermute | solution.py:341
  9.2 1.3 %collective-permute-start.8 = (bf16[40,2560]{1,0:T(8,128)(2,1)S(1)}, bf16[40,2560]{1,0:T(8,128)(2,1)S(1)}, u32[]{:S(2)}, u32[]{:S(2)}) collective-permute-start(bf16[40,2560]{1,0:T(8,128)(2,1)S(1)} %get-tuple-element.32), channel_id=1, source_target_pairs={{0,5},{1,4},{2,7},{3,6},{4,1},{5,0},{6,3},{7,2},{8,13},{9,12},{10,... | collective-permute-start | bytes 614408 | tf_op jit(solution)/shard_map/ppermute | solution.py:341
  10.5 2.2 %collective-permute-done.7.refs_4_ = bf16[40,2560]{1,0:T(8,128)(2,1)S(1)} collective-permute-done((bf16[40,2560]{1,0:T(8,128)(2,1)S(1)}, bf16[40,2560]{1,0:T(8,128)(2,1)S(1)}, u32[]{:S(2)}, u32[]{:S(2)}) %collective-permute-start.7) | collective-permute-done | bytes 204832 | tf_op jit(solution)/shard_map/ppermute | solution.py:341
  12.8 0.5 collective-permute-start
  13.2 0.0 collective-permute-done.4.refs_1_
  13.2 2.5 %collective-permute-start.1 = (bf16[40,2560]{1,0:T(8,128)(2,1)S(1)}, bf16[40,2560]{1,0:T(8,128)(2,1)S(1)}, u32[]{:S(2)}, u32[]{:S(2)}) collective-permute-start(bf16[40,2560]{1,0:T(8,128)(2,1)S(1)} %get-tuple-element.24), channel_id=1, source_target_pairs={{0,7},{1,6},{2,5},{3,4},{4,3},{5,2},{6,1},{7,0},{8,15},{9,14},{10,... | collective-permute-start | bytes 614408 | tf_op jit(solution)/shard_map/ppermute | solution.py:341
  15.8 4.3 %collective-permute-done.5.refs_2_ = bf16[40,2560]{1,0:T(8,128)(2,1)S(1)} collective-permute-done((bf16[40,2560]{1,0:T(8,128)(2,1)S(1)}, bf16[40,2560]{1,0:T(8,128)(2,1)S(1)}, u32[]{:S(2)}, u32[]{:S(2)}) %collective-permute-start.5) | collective-permute-done | bytes 204832 | tf_op jit(solution)/shard_map/ppermute | solution.py:341
  20.0 12.3 %collective-permute-done.6.refs_3_ = bf16[40,2560]{1,0:T(8,128)(2,1)S(1)} collective-permute-done((bf16[40,2560]{1,0:T(8,128)(2,1)S(1)}, bf16[40,2560]{1,0:T(8,128)(2,1)S(1)}, u32[]{:S(2)}, u32[]{:S(2)}) %collective-permute-start.6) | collective-permute-done | bytes 204832 | tf_op jit(solution)/shard_map/ppermute | solution.py:341
  32.3 0.0 collective-permute-done.8.refs_5_
  32.3 10.2 %shard_map.67 = (bf16[40,2560]{1,0:T(8,128)(2,1)S(1)}, bf16[40,2560]{1,0:T(8,128)(2,1)S(1)}, bf16[40,2560]{1,0:T(8,128)(2,1)S(1)}, bf16[40,2560]{1,0:T(8,128)(2,...) custom-call(bf16[40,2560]{1,0:T(8,128)(2,1)S(1)} %get-tuple-element.28.refs_0_, ...), custom_call_target="tpu_custom_call" | custom-call | flops 5662310400 | bytes 23592960 | tf_op jit(solution)/shard_map/pallas_call | solution.py:293
  42.5 0.6 collective-permute-start.9
  43.1 3.4 %collective-permute-start.10 = (bf16[40,2560]{1,0:T(8,128)(2,1)S(1)}, bf16[40,2560]{1,0:T(8,128)(2,1)S(1)}, u32[]{:S(2)}, u32[]{:S(2)}) collective-permute-start(bf16[40,2560]{1,0:T(8,128)(2,1)S(1)} %get-tuple-element.35), channel_id=1, source_target_pairs={{0,2},{1,3},{2,0},{3,1},{4,6},{5,7},{6,4},{7,5},{8,10},{9,11},{10,... | collective-permute-start | bytes 614408 | tf_op jit(solution)/shard_map/ppermute | solution.py:341
  46.5 0.0 collective-permute-start.11
  46.5 0.0 collective-permute-done.refs_0_
  46.5 2.9 %collective-permute-start.12 = (bf16[40,2560]{1,0:T(8,128)(2,1)S(1)}, bf16[40,2560]{1,0:T(8,128)(2,1)S(1)}, u32[]{:S(2)}, u32[]{:S(2)}) collective-permute-start(bf16[40,2560]{1,0:T(8,128)(2,1)S(1)} %get-tuple-element.37), channel_id=1, source_target_pairs={{0,4},{1,5},{2,6},{3,7},{4,0},{5,1},{6,2},{7,3},{8,12},{9,13},{10,... | collective-permute-start | bytes 614408 | tf_op jit(solution)/shard_map/ppermute | solution.py:341
  49.4 0.0 collective-permute-done.1.refs_1_
  49.4 0.0 copy-start
  49.4 0.0 copy-start.1
  49.4 1.1 %collective-permute-start.13 = (bf16[40,2560]{1,0:T(8,128)(2,1)S(1)}, bf16[40,2560]{1,0:T(8,128)(2,1)S(1)}, u32[]{:S(2)}, u32[]{:S(2)}) collective-permute-start(bf16[40,2560]{1,0:T(8,128)(2,1)S(1)} %get-tuple-element.38), channel_id=1, source_target_pairs={{0,5},{1,4},{2,7},{3,6},{4,1},{5,0},{6,3},{7,2},{8,13},{9,12},{10,... | collective-permute-start | bytes 614408 | tf_op jit(solution)/shard_map/ppermute | solution.py:341
  50.4 9.3 %shard_map.65 = (bf16[40,2560]{1,0:T(8,128)(2,1)S(1)}, bf16[40,2560]{1,0:T(8,128)(2,1)S(1)}) custom-call(bf16[40,2560]{1,0:T(8,128)(2,1)S(1)} %collective-permute-done.refs_0_, bf16[40,2560]{1,0:T(8,128)(2,1)S(1)} %collective-permute-done.1.refs_1_, bf16[2560,1536]{1,0:T(8,128)(2,1)} %refs_6_.1, bf16[2560,1536]{1,0:T(8,128)(2,1)} %refs_7_.1, ...), custom_call_target="tpu_custom_call" | custom-call | flops 1887436800 | bytes 23592960 | tf_op jit(solution)/shard_map/pallas_call | solution.py:293
  59.8 0.0 collective-permute-done.9.refs_2_
  59.8 1.4 %collective-permute-start.2 = (bf16[40,2560]{1,0:T(8,128)(2,1)S(1)}, bf16[40,2560]{1,0:T(8,128)(2,1)S(1)}, u32[]{:S(2)}, u32[]{:S(2)}) collective-permute-start(bf16[40,2560]{1,0:T(8,128)(2,1)S(1)} %get-tuple-element.25), channel_id=1, source_target_pairs={{0,6},{1,7},{2,4},{3,5},{4,2},{5,3},{6,0},{7,1},{8,14},{9,15},{10,... | collective-permute-start | bytes 614408 | tf_op jit(solution)/shard_map/ppermute | solution.py:341
  61.2 0.0 collective-permute-done.10.refs_3_
  61.2 0.6 collective-permute-start.3
  61.8 0.0 copy-done
  61.8 0.0 copy-done.1
  61.8 0.5 mixer.1
  62.4 0.0 collective-permute-done.11.refs_4_
  62.4 0.0 collective-permute-done.12.refs_5_
  62.4 12.5 %collective-permute-done.13.refs_6_ = bf16[40,2560]{1,0:T(8,128)(2,1)S(1)} collective-permute-done((bf16[40,2560]{1,0:T(8,128)(2,1)S(1)}, bf16[40,2560]{1,0:T(8,128)(2,1)S(1)}, u32[]{:S(2)}, u32[]{:S(2)}) %collective-permute-start.13) | collective-permute-done | bytes 204832 | tf_op jit(solution)/shard_map/ppermute | solution.py:341
  74.9 0.5 shard_map.68.refs_3_
  75.4 6.3 %collective-permute-done.2.refs_1_ = bf16[40,2560]{1,0:T(8,128)(2,1)S(1)} collective-permute-done((bf16[40,2560]{1,0:T(8,128)(2,1)S(1)}, bf16[40,2560]{1,0:T(8,128)(2,1)S(1)}, u32[]{:S(2)}, u32[]{:S(2)}) %collective-permute-start.2) | collective-permute-done | bytes 204832 | tf_op jit(solution)/shard_map/ppermute | solution.py:341
  81.7 3.3 %collective-permute-done.3.refs_2_ = bf16[40,2560]{1,0:T(8,128)(2,1)S(1)} collective-permute-done((bf16[40,2560]{1,0:T(8,128)(2,1)S(1)}, bf16[40,2560]{1,0:T(8,128)(2,1)S(1)}, u32[]{:S(2)}, u32[]{:S(2)}) %collective-permute-start.3) | collective-permute-done | bytes 204832 | tf_op jit(solution)/shard_map/ppermute | solution.py:341
  85.0 1.2 %shard_map.69 = bf16[128,2560]{1,0:T(8,128)(2,1)} custom-call(bf16[128,160]{1,0:T(8,128)(2,1)S(1)} %get-tuple-element.22.refs_0_, bf16[40,2560]{1,0:T(8,128)(2,1)S(1)} %collective-permute-done.2.refs_1_, bf16[40,2560]{1,0:T(8,128)(2,1)S(1)} %collective-permute-done.3.refs_2_, f32[128,2560]{1,0:T(8,128)S(1)} %shard_map.68.refs_3_), custom_call_target="tpu_custom_call" | custom-call | tf_op jit(solution)/shard_map/pallas_call | solution.py:317
Async XLA Ops:
  1.4 11.4 %collective-permute-start.7 = (bf16[40,2560]{1,0:T(8,128)(2,1)S(1)}, bf16[40,2560]{1,0:T(8,128)(2,1)S(1)}, u32[]{:S(2)}, u32[]{:S(2)}) collective-permute-start(bf16[40,2560]{1,0:T(8,128)(2,1)S(1)} %shard_map.66), channel_id=1, source_target_pairs={{0,4},{1,5},{2,6},{3,7},{4,0},{5,1},{6,2},{7,3},{8,12},{9,13},{10,... | collective-permute-start | bytes 614408 | tf_op jit(solution)/shard_map/ppermute | solution.py:341
  5.7 7.5 %collective-permute-start.4 = (bf16[40,2560]{1,0:T(8,128)(2,1)S(1)}, bf16[40,2560]{1,0:T(8,128)(2,1)S(1)}, u32[]{:S(2)}, u32[]{:S(2)}) collective-permute-start(bf16[40,2560]{1,0:T(8,128)(2,1)S(1)} %get-tuple-element.29), channel_id=1, source_target_pairs={{0,1},{1,0},{2,3},{3,2},{4,5},{5,4},{6,7},{7,6},{8,9},{9,8},{10,11... | collective-permute-start | bytes 614408 | tf_op jit(solution)/shard_map/ppermute | solution.py:341
  7.3 12.8 %collective-permute-start.5 = (bf16[40,2560]{1,0:T(8,128)(2,1)S(1)}, bf16[40,2560]{1,0:T(8,128)(2,1)S(1)}, u32[]{:S(2)}, u32[]{:S(2)}) collective-permute-start(bf16[40,2560]{1,0:T(8,128)(2,1)S(1)} %get-tuple-element.30), channel_id=1, source_target_pairs={{0,2},{1,3},{2,0},{3,1},{4,6},{5,7},{6,4},{7,5},{8,10},{9,11},{10,... | collective-permute-start | bytes 614408 | tf_op jit(solution)/shard_map/ppermute | solution.py:341
  7.7 24.6 %collective-permute-start.6 = (bf16[40,2560]{1,0:T(8,128)(2,1)S(1)}, bf16[40,2560]{1,0:T(8,128)(2,1)S(1)}, u32[]{:S(2)}, u32[]{:S(2)}) collective-permute-start(bf16[40,2560]{1,0:T(8,128)(2,1)S(1)} %get-tuple-element.31), channel_id=1, source_target_pairs={{0,3},{1,2},{2,1},{3,0},{4,7},{5,6},{6,5},{7,4},{8,11},{9,10},{10,... | collective-permute-start | bytes 614408 | tf_op jit(solution)/shard_map/ppermute | solution.py:341
  9.2 23.1 %collective-permute-start.8 = (bf16[40,2560]{1,0:T(8,128)(2,1)S(1)}, bf16[40,2560]{1,0:T(8,128)(2,1)S(1)}, u32[]{:S(2)}, u32[]{:S(2)}) collective-permute-start(bf16[40,2560]{1,0:T(8,128)(2,1)S(1)} %get-tuple-element.32), channel_id=1, source_target_pairs={{0,5},{1,4},{2,7},{3,6},{4,1},{5,0},{6,3},{7,2},{8,13},{9,12},{10,... | collective-permute-start | bytes 614408 | tf_op jit(solution)/shard_map/ppermute | solution.py:341
  12.8 33.7 %collective-permute-start = (bf16[40,2560]{1,0:T(8,128)(2,1)S(1)}, bf16[40,2560]{1,0:T(8,128)(2,1)S(1)}, u32[]{:S(2)}, u32[]{:S(2)}) collective-permute-start(bf16[40,2560]{1,0:T(8,128)(2,1)S(1)} %get-tuple-element.23), channel_id=1, source_target_pairs={{0,6},{1,7},{2,4},{3,5},{4,2},{5,3},{6,0},{7,1},{8,14},{9,15},{10,... | collective-permute-start | bytes 614408 | tf_op jit(solution)/shard_map/ppermute | solution.py:341
  13.2 36.1 %collective-permute-start.1 = (bf16[40,2560]{1,0:T(8,128)(2,1)S(1)}, bf16[40,2560]{1,0:T(8,128)(2,1)S(1)}, u32[]{:S(2)}, u32[]{:S(2)}) collective-permute-start(bf16[40,2560]{1,0:T(8,128)(2,1)S(1)} %get-tuple-element.24), channel_id=1, source_target_pairs={{0,7},{1,6},{2,5},{3,4},{4,3},{5,2},{6,1},{7,0},{8,15},{9,14},{10,... | collective-permute-start | bytes 614408 | tf_op jit(solution)/shard_map/ppermute | solution.py:341
  42.5 17.3 %collective-permute-start.9 = (bf16[40,2560]{1,0:T(8,128)(2,1)S(1)}, bf16[40,2560]{1,0:T(8,128)(2,1)S(1)}, u32[]{:S(2)}, u32[]{:S(2)}) collective-permute-start(bf16[40,2560]{1,0:T(8,128)(2,1)S(1)} %get-tuple-element.34), channel_id=1, source_target_pairs={{0,1},{1,0},{2,3},{3,2},{4,5},{5,4},{6,7},{7,6},{8,9},{9,8},{10,11... | collective-permute-start | bytes 614408 | tf_op jit(solution)/shard_map/ppermute | solution.py:341
  43.1 18.2 %collective-permute-start.10 = (bf16[40,2560]{1,0:T(8,128)(2,1)S(1)}, bf16[40,2560]{1,0:T(8,128)(2,1)S(1)}, u32[]{:S(2)}, u32[]{:S(2)}) collective-permute-start(bf16[40,2560]{1,0:T(8,128)(2,1)S(1)} %get-tuple-element.35), channel_id=1, source_target_pairs={{0,2},{1,3},{2,0},{3,1},{4,6},{5,7},{6,4},{7,5},{8,10},{9,11},{10,... | collective-permute-start | bytes 614408 | tf_op jit(solution)/shard_map/ppermute | solution.py:341
  46.5 15.9 %collective-permute-start.11 = (bf16[40,2560]{1,0:T(8,128)(2,1)S(1)}, bf16[40,2560]{1,0:T(8,128)(2,1)S(1)}, u32[]{:S(2)}, u32[]{:S(2)}) collective-permute-start(bf16[40,2560]{1,0:T(8,128)(2,1)S(1)} %get-tuple-element.36), channel_id=1, source_target_pairs={{0,3},{1,2},{2,1},{3,0},{4,7},{5,6},{6,5},{7,4},{8,11},{9,10},{10,... | collective-permute-start | bytes 614408 | tf_op jit(solution)/shard_map/ppermute | solution.py:341
  46.5 15.9 %collective-permute-start.12 = (bf16[40,2560]{1,0:T(8,128)(2,1)S(1)}, bf16[40,2560]{1,0:T(8,128)(2,1)S(1)}, u32[]{:S(2)}, u32[]{:S(2)}) collective-permute-start(bf16[40,2560]{1,0:T(8,128)(2,1)S(1)} %get-tuple-element.37), channel_id=1, source_target_pairs={{0,4},{1,5},{2,6},{3,7},{4,0},{5,1},{6,2},{7,3},{8,12},{9,13},{10,... | collective-permute-start | bytes 614408 | tf_op jit(solution)/shard_map/ppermute | solution.py:341
  49.4 12.5 %copy-start = (s32[128,2]{0,1:T(2,128)S(1)}, s32[128,2]{0,1:T(2,128)}, u32[]{:S(2)}) copy-start(s32[128,2]{0,1:T(2,128)} %param.7) | copy-start | bytes 3076
  49.4 12.5 %copy-start.1 = (f32[128,2]{0,1:T(2,128)S(1)}, f32[128,2]{0,1:T(2,128)}, u32[]{:S(2)}) copy-start(f32[128,2]{0,1:T(2,128)} %param.8) | copy-start | bytes 3076
  49.4 25.5 %collective-permute-start.13 = (bf16[40,2560]{1,0:T(8,128)(2,1)S(1)}, bf16[40,2560]{1,0:T(8,128)(2,1)S(1)}, u32[]{:S(2)}, u32[]{:S(2)}) collective-permute-start(bf16[40,2560]{1,0:T(8,128)(2,1)S(1)} %get-tuple-element.38), channel_id=1, source_target_pairs={{0,5},{1,4},{2,7},{3,6},{4,1},{5,0},{6,3},{7,2},{8,13},{9,12},{10,... | collective-permute-start | bytes 614408 | tf_op jit(solution)/shard_map/ppermute | solution.py:341
  59.8 21.9 %collective-permute-start.2 = (bf16[40,2560]{1,0:T(8,128)(2,1)S(1)}, bf16[40,2560]{1,0:T(8,128)(2,1)S(1)}, u32[]{:S(2)}, u32[]{:S(2)}) collective-permute-start(bf16[40,2560]{1,0:T(8,128)(2,1)S(1)} %get-tuple-element.25), channel_id=1, source_target_pairs={{0,6},{1,7},{2,4},{3,5},{4,2},{5,3},{6,0},{7,1},{8,14},{9,15},{10,... | collective-permute-start | bytes 614408 | tf_op jit(solution)/shard_map/ppermute | solution.py:341
  61.2 23.8 %collective-permute-start.3 = (bf16[40,2560]{1,0:T(8,128)(2,1)S(1)}, bf16[40,2560]{1,0:T(8,128)(2,1)S(1)}, u32[]{:S(2)}, u32[]{:S(2)}) collective-permute-start(bf16[40,2560]{1,0:T(8,128)(2,1)S(1)} %get-tuple-element.26), channel_id=1, source_target_pairs={{0,7},{1,6},{2,5},{3,4},{4,3},{5,2},{6,1},{7,0},{8,15},{9,14},{10,... | collective-permute-start | bytes 614408 | tf_op jit(solution)/shard_map/ppermute | solution.py:341
